TPU v7x, 32 devices: a whole 2x2x4 slice. The times are simulated.
32 devices in a mesh: sp: 16 (over z, x, core), tp: 2 (over y).
Axes of the slice: x: 2, y: 2, z: 4, core: 2. Of those that a mesh axis runs over, the one named last changes fastest.
Arguments:
- activations: bfloat16 [2, 2048, 8192], P(None, 'sp', 'tp'), may hold values from -250 to 250
- norm_gain: bfloat16 [8192], P('tp'), may hold values from 0.5 to 1.5
- keep_bits: int32 [2, 2048, 1024], P(None, 'sp', 'tp'), may hold values from 0 to 255, as said below
- key_value_weight: bfloat16 [1024, 8192], P('sp', 'tp'), may hold values from -0.0625 to 0.0625
- queries: bfloat16 [2, 2048, 4096], P('tp', 'sp'), may hold values from -68 to 68
- segment: int32 [4096], replicated, may hold values from 0 to 15, never falling along the last dimension, each value on 1 to 512 neighbouring positions
- cotangent: bfloat16 [2, 2048, 4096], P('tp', 'sp'), may hold values from -12 to 12
Outputs:
- attended: bfloat16 [2, 2048, 4096], P('tp', 'sp')
- grad_queries: bfloat16 [2, 2048, 4096], P('tp', 'sp')
- grad_activations: bfloat16 [2, 2048, 8192], P(None, 'sp', 'tp')
- grad_weight: float32 [1024, 8192], P('sp', 'tp')
- grad_gain: float32 [8192], P('tp')
Inputs may be any that keep to these rules, and one draw needn't show every extreme that they name: Bit j of keep_bits[a, b, w] is the keep flag of feature 8 w + j. segment numbers never fall along the sequence; each document covers 1 to 512 positions, and one covers exactly 512.
All inputs are finite; a program needn't handle non-finite values.
Results may differ from a plain program's by a relative error of at most 0.012.
The roundings to bfloat16 on the way count: a program that leaves them out, or rounds other values in their place, can miss the bound.
Values may be sent and summed in bfloat16 or wider, within the bound.
A program may use at most 128 MiB of HBM per device.

v0:
```python
import functools

import jax
import jax.numpy as jnp
import numpy as np
from jax import lax
from jax.experimental import pallas as pl
from jax.experimental.pallas import tpu as pltpu
from jax.sharding import PartitionSpec as P

D = 8192
HQ = 32
KVH = 4
HD = 128
DOC = 512
GROUP = 8
EPS = 1e-05
KEEP_RATE = 0.9
MASKED_SCORE = -1e30
SCALE = HD ** (-0.5)
DROP = float(np.float32(1.0) / np.float32(KEEP_RATE))
KV = 2 * HD
F32 = jnp.float32
BF16 = jnp.bfloat16
NT = (((1,), (1,)), ((), ()))
TN = (((0,), (0,)), ((), ()))


class Links:
    def __init__(self, send_sems):
        self.send_sems = send_sems
        self.pending = []

    def send(self, cond, src, dst, recv_sem, sp, tp):
        sem = self.send_sems.at[len(self.pending)]

        def make():
            return pltpu.make_async_remote_copy(
                src_ref=src,
                dst_ref=dst,
                send_sem=sem,
                recv_sem=recv_sem,
                device_id={"sp": sp, "tp": tp},
                device_id_type=pl.DeviceIdType.MESH,
            )

        self.pending.append((cond, make))
        when(cond, lambda: make().start())

    def arrive(self, dst, recv_sem, sp, tp):
        pltpu.make_async_remote_copy(
            src_ref=dst,
            dst_ref=dst,
            send_sem=self.send_sems.at[0],
            recv_sem=recv_sem,
            device_id={"sp": sp, "tp": tp},
            device_id_type=pl.DeviceIdType.MESH,
        ).wait_recv()

    def drain(self):
        for cond, make in self.pending:
            when(cond, lambda: make().wait_send())


def when(cond, body):
    if cond is True:
        body()
    else:
        pl.when(cond)(body)


def step_kernel(
    shape, x_ref, gain_ref, bits_ref, w_ref, query_ref, seg_ref, cot_ref,
    att_ref, gq_ref, ga_ref, gw_ref, gg_ref,
    wfull, hall, mask, inv, squares, dots, kvp, kvr, kvh, rim, rimr, own_grad, dkvall, dkt,
    own32, xsend, xr, zs, zru, zrd, ups, gains, probs, grads,
    send_sems, w_sem, w_recv, h_recv, sq_recv, dot_recv, kv_recv, halo_recv, rim_recv, dkv_recv, dkc_recv,
    x_recv, up_recv, down_recv, gain_recv,
):
    S, T, X, Z, rows, F, WR, halo = shape
    R = T * rows
    places = S * T
    sp, tp = lax.axis_index("sp"), lax.axis_index("tp")
    c = sp % 2
    x = sp // 2 % X
    z = sp // (2 * X)
    place = tp * S + sp
    at = lambda zz, xx, cc: (zz * X + xx) * 2 + cc
    mate = at(z, x, 1 - c)
    links = Links(send_sems)

    fetch = pltpu.make_async_copy(w_ref, wfull.at[sp], w_sem)
    fetch.start()
    fetch.wait()

    def spread(cond, zz):
        for k in range(1, X):
            links.send(cond, wfull.at[at(zz, x, c)], wfull.at[at(zz, x, c)], w_recv.at[at(zz, x, c)], at(z, (x + k) % X, c), tp)
        links.send(cond, wfull.at[at(zz, x, c)], wfull.at[at(zz, x, c)], w_recv.at[at(zz, x, c)], mate, tp)

    def pass_on(cond, zz, step):
        block = at(zz, x, c)
        links.send(cond, wfull.at[block], wfull.at[block], w_recv.at[block], at(z + step, x, c), tp)

    pass_on(z < Z - 1, z, 1)
    pass_on(z > 0, z, -1)
    spread(True, z)

    strip = 16
    lanes = F // 128

    def square_rows(i, _):
        r = pl.ds(pl.multiple_of(i * strip, strip), strip)
        wide = x_ref[r, :].astype(F32)
        wide = wide * wide
        total = wide[:, :128]
        for k in range(1, lanes):
            total = total + wide[:, k * 128 : (k + 1) * 128]
        squares[tp, r, :] = total
        return 0

    lax.fori_loop(0, R // strip, square_rows, 0)
    for k in range(1, T):
        links.send(True, squares.at[tp], squares.at[tp], sq_recv.at[tp], sp, (tp + k) % T)

    words = min(128, F // 8)
    lane = lax.broadcasted_iota(jnp.int32, (words, words * 8), 1)
    expand = (lane // 8 == lax.broadcasted_iota(jnp.int32, (words, words * 8), 0)).astype(F32).astype(BF16)
    shifts = lax.broadcasted_iota(jnp.int32, (rows, words * 8), 1) % 8
    for w in range(F // 8 // words):
        def unpack(i, _):
            r = pl.ds(pl.multiple_of(i * rows, rows), rows)
            word = bits_ref[r, w * words : (w + 1) * words].astype(F32).astype(BF16)
            wide = jnp.dot(word, expand, preferred_element_type=F32).astype(jnp.int32)
            flag = jnp.bitwise_and(jnp.right_shift(wide, shifts), 1)
            mask[r, w * words * 8 : (w + 1) * words * 8] = flag.astype(F32).astype(BF16)
            return 0
        lax.fori_loop(0, T, unpack, 0)

    for k in range(1, T):
        links.arrive(squares.at[(tp + k) % T], sq_recv.at[(tp + k) % T], sp, (tp + k) % T)

    def norm_rows(i, _):
        r = pl.ds(pl.multiple_of(i * strip, strip), strip)
        total = squares[0, r, :]
        for t in range(1, T):
            total = total + squares[t, r, :]
        inv_rms = lax.rsqrt(jnp.sum(total, axis=1, keepdims=True) / D + EPS)
        inv[r, :] = jnp.broadcast_to(inv_rms, (strip, 128))
        wide = x_ref[r, :].astype(F32) * inv_rms * gain_ref[...].astype(F32)
        hall[c, r, :] = (wide * (mask[r, :].astype(F32) * DROP)).astype(BF16)
        return 0

    lax.fori_loop(0, R // strip, norm_rows, 0)
    links.send(True, hall.at[c], hall.at[c], h_recv, mate, tp)

    def project(g):
        weight = wfull[pl.ds(g * 2 * X, 2 * X)].reshape(2 * X * WR, F)
        part = lax.dot_general(hall[c], weight, NT, preferred_element_type=F32)
        for t in range(T):
            kvp[g, t] = part[t * rows : (t + 1) * rows]

    def reached(g):
        for k in range(1, X):
            block = at(g, (x + k) % X, c)
            links.arrive(wfull.at[block], w_recv.at[block], mate, tp)

    def across(cond, g):
        for k in range(1, X):
            block = at(g, (x + k) % X, c)
            links.send(cond, wfull.at[block], wfull.at[block], w_recv.at[block], mate, tp)

    def complete(cond, g):
        def body():
            for k in range(X):
                block = at(g, (x + k) % X, 1 - c)
                links.arrive(wfull.at[block], w_recv.at[block], mate, tp)
            project(g)
        when(cond, body)
        for k in range(1, T):
            to = (tp + k) % T
            links.send(cond, kvp.at[g, to], kvr.at[g, tp], kv_recv.at[g, tp], sp, to)

    steps = [(0, 0)] + [(d, s) for d in range(1, Z) for s in (-1, 1)]

    def group_of(step):
        d, s = step
        g = z + d * s
        return (True if d == 0 else (g >= 0) & (g < Z)), g

    for i in range(1, len(steps) + 2):
        if i < len(steps):
            cond, g = group_of(steps[i])
            s = steps[i][1]
            block = at(g, x, c)
            when(cond, lambda: links.arrive(wfull.at[block], w_recv.at[block], mate, tp))
            pass_on(cond & (z - s >= 0) & (z - s < Z), g, -s)
            spread(cond, g)
        if i >= 2:
            cond, g = group_of(steps[i - 2])
            when(cond, lambda: reached(g))
            across(cond, g)
            complete(cond, g)

    for g in range(KVH):
        total = kvp[g, tp]
        for k in range(1, T):
            other = (tp + k) % T
            links.arrive(kvr.at[g, other], kv_recv.at[g, other], sp, other)
            total = total + kvr[g, other]
        kvh[halo, g] = total.astype(BF16)
    for d in range(1, halo + 1):
        to = place + d
        links.send(to < places, kvh.at[halo], kvh.at[halo - d], halo_recv.at[halo - d], to % S, to // S % T)

    def blank(d):
        kvh[halo - d] = jnp.zeros(kvh.shape[1:], BF16)

    for d in range(1, halo + 1):
        pl.when(place < d)(functools.partial(blank, d))
    seg_rows = []
    for j in range(halo + 1):
        back = place - (halo - j)
        row = seg_ref[pl.ds(jnp.maximum(back, 0), 1), :]
        seg_rows.append(jnp.where(back >= 0, row, -1))
    for d in range(1, halo + 1):
        def got(d=d):
            links.arrive(kvh.at[halo - d], halo_recv.at[halo - d], mate, tp)
        pl.when(place >= d)(got)

    keys = rows * (halo + 1)
    seg_keys = jnp.concatenate(seg_rows, axis=1)
    seg_query = jnp.transpose(jnp.broadcast_to(seg_rows[halo].astype(F32), (rows, rows)))[:, :1]
    position = lax.broadcasted_iota(jnp.int32, (rows, keys), 0) + halo * rows
    other = lax.broadcasted_iota(jnp.int32, (rows, keys), 1)
    bias = jnp.where((other <= position) & (seg_query == seg_keys.astype(F32)), 0.0, MASKED_SCORE)

    def attend(g, _):
        pair = kvh[:, g].reshape(keys, KV)
        key_part, value_part = pair[:, :HD], pair[:, HD:]
        queries, cots = [], []
        for n in range(GROUP):
            columns = pl.ds(pl.multiple_of((g * GROUP + n) * HD, HD), HD)
            query, grad = query_ref[:, columns], cot_ref[:, columns]
            queries.append(query)
            cots.append(grad)
            scores = lax.dot_general(query, key_part, NT, preferred_element_type=F32) * SCALE
            scores = jnp.where(bias == 0.0, scores, MASKED_SCORE)
            weights = jnp.exp(scores - jnp.max(scores, axis=1, keepdims=True))
            prob = weights / jnp.sum(weights, axis=1, keepdims=True)
            low = prob.astype(BF16)
            att_ref[:, columns] = jnp.dot(low, value_part, preferred_element_type=F32).astype(BF16)
            grad_prob = lax.dot_general(grad, value_part, NT, preferred_element_type=F32)
            inner = jnp.sum(prob * grad_prob, axis=1, keepdims=True)
            grad_score = (prob * (grad_prob - inner)).astype(BF16)
            gq_ref[:, columns] = (jnp.dot(grad_score, key_part, preferred_element_type=F32) * SCALE).astype(BF16)
            probs[n * rows : (n + 1) * rows, :] = low
            grads[n * rows : (n + 1) * rows, :] = grad_score
        grad_key = lax.dot_general(grads[...], jnp.concatenate(queries, axis=0), TN, preferred_element_type=F32) * SCALE
        grad_value = lax.dot_general(probs[...], jnp.concatenate(cots, axis=0), TN, preferred_element_type=F32)
        for j in range(halo):
            r = slice(j * rows, (j + 1) * rows)
            rim[j, g, :, :HD] = grad_key[r].astype(BF16)
            rim[j, g, :, HD:] = grad_value[r].astype(BF16)
        own_grad[g, :, :HD] = grad_key[halo * rows :]
        own_grad[g, :, HD:] = grad_value[halo * rows :]
        return 0

    lax.fori_loop(0, KVH, attend, 0)

    for d in range(1, halo + 1):
        to = place - d
        links.send(to >= 0, rim.at[halo - d], rimr.at[d - 1], rim_recv.at[d - 1], (to + places) % S, (to + places) // S % T)
    for d in range(1, halo + 1):
        def add(d=d):
            links.arrive(rimr.at[d - 1], rim_recv.at[d - 1], mate, tp)
            for g in range(KVH):
                own_grad[g] = own_grad[g] + rimr[d - 1, g].astype(F32)
        pl.when(place + d < places)(add)
    for g in range(KVH):
        dkvall[c, tp, g] = own_grad[g].astype(BF16)
    for k in range(1, T):
        links.send(True, dkvall.at[c, tp], dkvall.at[c, tp], dkv_recv.at[tp], sp, (tp + k) % T)
    links.send(True, dkvall.at[c, tp], dkvall.at[c, tp], dkc_recv.at[tp], mate, tp)
    for k in range(1, T):
        other = (tp + k) % T
        links.arrive(dkvall.at[c, other], dkv_recv.at[other], sp, other)
        links.send(True, dkvall.at[c, other], dkvall.at[c, other], dkc_recv.at[other], mate, tp)
    for k in range(T):
        other = (tp + k) % T
        links.arrive(dkvall.at[1 - c, other], dkc_recv.at[other], mate, tp)
    links.arrive(hall.at[1 - c], h_recv, mate, tp)

    order = [g for pair in zip(range(Z // 2), range(Z - 1, Z // 2 - 1, -1)) for g in pair]
    tile = min(512, F)
    for g in order:
        dkt[g] = jnp.transpose(dkvall[:, :, g].reshape(2 * R, KV).astype(F32)).astype(BF16)
        left = jnp.concatenate(
            [dkt[g, pl.ds(pl.multiple_of(((x + k) % X * 2 + c) * WR, WR), WR), :] for k in range(X)], axis=0
        )

        def outer(i, _, g=g, left=left):
            columns = pl.ds(pl.multiple_of(i * tile, tile), tile)
            right = hall[:, :, columns].reshape(2 * R, tile)
            part = jnp.dot(left, right, preferred_element_type=F32)
            own32[g, :, columns] = part[:WR]
            for k in range(1, X):
                xsend[g, k - 1, :, columns] = part[k * WR : (k + 1) * WR].astype(BF16)
            return 0

        lax.fori_loop(0, F // tile, outer, 0)
        for k in range(1, X):
            links.send(True, xsend.at[g, k - 1], xr.at[g, k - 1], x_recv.at[g, k - 1], at(z, (x + k) % X, c), tp)

    dkv_mine = jnp.concatenate([dkvall[c, :, g].reshape(R, KV) for g in range(KVH)], axis=1)
    dots[tp] = jnp.zeros((R, 128), F32)
    inv_column = inv[:, :1]

    def hidden(i, _):
        columns = pl.ds(pl.multiple_of(i * tile, tile), tile)
        weight = wfull[:, :, columns].reshape(S * WR, tile)
        scaled = jnp.dot(dkv_mine, weight, preferred_element_type=F32) * (mask[:, columns].astype(F32) * DROP)
        wide = x_ref[:, columns].astype(F32)
        gains[0, :, columns] = jnp.sum(scaled * wide * inv_column, axis=0, keepdims=True)
        upstream = scaled * gain_ref[:, columns].astype(F32)
        ups[:, columns] = upstream
        upstream = upstream * wide
        total = upstream[:, :128]
        for k in range(1, tile // 128):
            total = total + upstream[:, k * 128 : (k + 1) * 128]
        dots[tp] = dots[tp] + total
        return 0

    lax.fori_loop(0, F // tile, hidden, 0)
    for k in range(1, T):
        links.send(True, dots.at[tp], dots.at[tp], dot_recv.at[tp], sp, (tp + k) % T)
    links.send(True, gains.at[0], gains.at[1], gain_recv.at[1], mate, tp)
    links.arrive(gains.at[1], gain_recv.at[1], mate, tp)
    gains[2] = gains[0] + gains[1]
    for k in range(1, X):
        links.send(True, gains.at[2], gains.at[2 + k], gain_recv.at[2 + k], at(z, (x + k) % X, c), tp)
    total = gains[2]
    for k in range(1, X):
        links.arrive(gains.at[2 + k], gain_recv.at[2 + k], mate, tp)
        total = total + gains[2 + k]
    gains[2 + X] = total
    for k in range(1, Z):
        links.send(True, gains.at[2 + X], gains.at[2 + X + k], gain_recv.at[2 + X + k], at((z + k) % Z, x, c), tp)

    for k in range(1, T):
        links.arrive(dots.at[(tp + k) % T], dot_recv.at[(tp + k) % T], sp, (tp + k) % T)

    def finish_rows(i, _):
        r = pl.ds(pl.multiple_of(i * strip, strip), strip)
        total = dots[0, r, :]
        for t in range(1, T):
            total = total + dots[t, r, :]
        row_dot = jnp.sum(total, axis=1, keepdims=True)
        scale = inv[r, :1]
        ga_ref[r, :] = (
            scale * ups[r, :] - x_ref[r, :].astype(F32) * ((scale * scale * scale) * row_dot / D)
        ).astype(BF16)
        return 0

    lax.fori_loop(0, R // strip, finish_rows, 0)

    norm = (places * rows) ** (-0.5)
    for k in range(1, Z):
        links.arrive(gains.at[2 + X + k], gain_recv.at[2 + X + k], mate, tp)
        total = total + gains[2 + X + k]
    gg_ref[...] = total * norm

    def fold(g, extra, out):
        def body(i, _):
            columns = pl.ds(pl.multiple_of(i * tile, tile), tile)
            value = own32[g, :, columns]
            for ref in extra:
                value = value + ref[:, columns].astype(F32)
            out(columns, value)
            return 0
        lax.fori_loop(0, F // tile, body, 0)

    def keep_low(g, columns, value):
        zs[g, :, columns] = value.astype(BF16)

    def keep(g, columns, value):
        own32[g, :, columns] = value

    for g in order:
        for k in range(1, X):
            links.arrive(xr.at[g, k - 1], x_recv.at[g, k - 1], mate, tp)
        parts = [xr.at[g, k - 1] for k in range(1, X)]

        def incoming(ref, sem, g=g, parts=parts):
            links.arrive(ref.at[g], sem.at[g], mate, tp)
            fold(g, parts + [ref.at[g]], functools.partial(keep_low, g))

        pl.when(((z < g) & (z == 0)) | ((z > g) & (z == Z - 1)))(lambda: fold(g, parts, functools.partial(keep_low, g)))
        pl.when((z < g) & (z > 0))(lambda: incoming(zru, up_recv))
        pl.when((z > g) & (z < Z - 1))(lambda: incoming(zrd, down_recv))
        pl.when(z == g)(lambda: fold(g, parts, functools.partial(keep, g)))
        links.send(z < g, zs.at[g], zru.at[g], up_recv.at[g], at(z + 1, x, c), tp)
        links.send(z > g, zs.at[g], zrd.at[g], down_recv.at[g], at(z - 1, x, c), tp)

    def result(columns, value):
        gw_ref[:, columns] = value * norm

    pl.when(z > 0)(lambda: links.arrive(zru.at[z], up_recv.at[z], mate, tp))
    pl.when(z < Z - 1)(lambda: links.arrive(zrd.at[z], down_recv.at[z], mate, tp))
    pl.when(z == 0)(lambda: fold(z, [zrd.at[z]], result))
    pl.when(z == Z - 1)(lambda: fold(z, [zru.at[z]], result))
    pl.when((z > 0) & (z < Z - 1))(lambda: fold(z, [zru.at[z], zrd.at[z]], result))
    links.drain()


def on_device(activations, norm_gain, keep_bits, key_value_weight, queries, segment, cotangent):
    S, T = lax.axis_size("sp"), lax.axis_size("tp")
    blocks, rows, F = activations.shape
    WR = key_value_weight.shape[0]
    Z = KVH
    X = S // (2 * Z)
    R = blocks * rows
    halo = -(-(DOC - 1) // rows)
    keys = rows * (halo + 1)
    shape = (S, T, X, Z, rows, F, WR, halo)
    vmem = pl.BlockSpec(memory_space=pltpu.VMEM)
    dma = pltpu.SemaphoreType.DMA
    wide = queries.shape[-1]
    out = pl.pallas_call(
        functools.partial(step_kernel, shape),
        in_specs=[vmem, vmem, vmem, pl.BlockSpec(memory_space=pl.ANY), vmem, vmem, vmem],
        out_specs=[vmem] * 5,
        out_shape=[
            jax.ShapeDtypeStruct((rows, wide), BF16),
            jax.ShapeDtypeStruct((rows, wide), BF16),
            jax.ShapeDtypeStruct((R, F), BF16),
            jax.ShapeDtypeStruct((WR, F), F32),
            jax.ShapeDtypeStruct((1, F), F32),
        ],
        scratch_shapes=[
            pltpu.VMEM((S, WR, F), BF16),
            pltpu.VMEM((2, R, F), BF16),
            pltpu.VMEM((R, F), BF16),
            pltpu.VMEM((R, 128), F32),
            pltpu.VMEM((T, R, 128), F32),
            pltpu.VMEM((T, R, 128), F32),
            pltpu.VMEM((KVH, T, rows, KV), F32),
            pltpu.VMEM((KVH, T, rows, KV), F32),
            pltpu.VMEM((halo + 1, KVH, rows, KV), BF16),
            pltpu.VMEM((halo, KVH, rows, KV), BF16),
            pltpu.VMEM((halo, KVH, rows, KV), BF16),
            pltpu.VMEM((KVH, rows, KV), F32),
            pltpu.VMEM((2, T, KVH, rows, KV), BF16),
            pltpu.VMEM((KVH, KV, 2 * R), BF16),
            pltpu.VMEM((Z, WR, F), F32),
            pltpu.VMEM((Z, X - 1, WR, F), BF16),
            pltpu.VMEM((Z, X - 1, WR, F), BF16),
            pltpu.VMEM((Z, WR, F), BF16),
            pltpu.VMEM((Z, WR, F), BF16),
            pltpu.VMEM((Z, WR, F), BF16),
            pltpu.VMEM((R, F), F32),
            pltpu.VMEM((2 + X + Z, 1, F), F32),
            pltpu.VMEM((GROUP * rows, keys), BF16),
            pltpu.VMEM((GROUP * rows, keys), BF16),
            dma((240,)),
            dma,
            dma((S,)),
            dma,
            dma((T,)),
            dma((T,)),
            dma((KVH, T)),
            dma((halo,)),
            dma((halo,)),
            dma((T,)),
            dma((T,)),
            dma((Z, X)),
            dma((Z,)),
            dma((Z,)),
            dma((2 + X + Z,)),
        ],
        compiler_params=pltpu.CompilerParams(has_side_effects=True, vmem_limit_bytes=63 * 2**20),
    )(
        activations.reshape(R, F),
        norm_gain.reshape(1, F),
        keep_bits.reshape(R, F // 8),
        key_value_weight,
        queries[0],
        segment.reshape(S * T, rows),
        cotangent[0],
    )
    attended, grad_queries, grad_activations, grad_weight, grad_gain = out
    return (
        attended[None],
        grad_queries[None],
        grad_activations.reshape(activations.shape),
        grad_weight,
        grad_gain.reshape(F),
    )


def solution(mesh):
    return jax.shard_map(
        on_device,
        mesh=mesh,
        in_specs=(
            P(None, "sp", "tp"),
            P("tp"),
            P(None, "sp", "tp"),
            P("sp", "tp"),
            P("tp", "sp", None),
            P(),
            P("tp", "sp", None),
        ),
        out_specs=(
            P("tp", "sp", None),
            P("tp", "sp", None),
            P(None, "sp", "tp"),
            P("sp", "tp"),
            P("tp"),
        ),
        check_vma=False,
    )
```

profile of v0, /device:TPU:12, one launch (start us, length us, event | category | flops | bytes accessed | tf_op | source)
XLA Modules:
  0.0 263.9 jit_solution(13302501257061514203)
XLA Ops:
  0.6 1.3 reshape.29.gain_ref
  1.9 255.0 %shard_map.110 = (bf16[128,4096]{1,0:T(8,128)(2,1)}, bf16[128,4096]{1,0:T(8,128)(2,1)}, bf16[256,4096]{1,0:T(8,128)(2,1)}, f32[64,4096]{1,0:T(8,128)}, f32[1,4096]{1,0:T(1,128)}) custom-call(bf16[256,4096]{1,0:T(8,128)(2,1)} %bitcast.9, bf16[1,4096]{1,0:T(2,128)(2,1)} %reshape.29.gain_ref, s32[256,512]{1,0:T(8,128)} %bitcast.15, bf16[64,4096]{1,0:T(8,128)(2,1)} %w_ref.1, ...), custom_call_target="tpu_custom_call" | custom-call | tf_op jit(solution)/shard_map/pallas_call | solution.py:429
  256.9 0.0 copy-start.2
  256.9 0.0 copy-start
  256.9 2.4 copy.17
  259.4 0.0 copy-done.2
  259.4 1.0 copy.18
  260.4 0.0 copy-done
  260.4 0.0 copy-start.1
  260.4 1.3 copy.19
  261.7 0.6 copy-done.1
  262.3 0.0 copy-start.3
  262.3 1.0 copy.20
  263.3 0.0 copy-done.3
  263.3 0.6 copy.21
Async XLA Ops:
  256.9 2.5 copy-start.2
  256.9 3.4 %copy-start = (bf16[256,4096]{1,0:T(8,128)(2,1)S(1)}, bf16[256,4096]{1,0:T(8,128)(2,1)}, u32[]{:S(2)}) copy-start(bf16[256,4096]{1,0:T(8,128)(2,1)} %get-tuple-element.12) | copy-start | bytes 6291460
  260.4 2.0 copy-start.1
  262.3 1.0 copy-start.3
where the time goes:
time: 269 us; the launch traced here: 264 us
  Pallas kernels  255 us (95%)
  local copies, waits for them, and re-layouts  8.27 us (3%)
    pallas_call x1, Pallas kernels, on_device(): pl.pallas_call(functools.partial(step_kernel, shape), in_specs=[vmem, vme...  255 us
    unnamed x13, local copies, waits for them, and re-layouts  6.95 us

commit v1 on v0

v1 whole, which is shorter than its diff:
```python
import functools

import jax
import jax.numpy as jnp
import numpy as np
from jax import lax
from jax.experimental import pallas as pl
from jax.experimental.pallas import tpu as pltpu
from jax.sharding import PartitionSpec as P

D = 8192
HQ = 32
KVH = 4
HD = 128
DOC = 512
GROUP = 8
EPS = 1e-05
KEEP_RATE = 0.9
MASKED_SCORE = -1e30
SCALE = HD ** (-0.5)
DROP = float(np.float32(1.0) / np.float32(KEEP_RATE))
KV = 2 * HD
F32 = jnp.float32
BF16 = jnp.bfloat16
NT = (((1,), (1,)), ((), ()))
UNROLL = 2
TN = (((0,), (0,)), ((), ()))


class Links:
    def __init__(self, send_sems):
        self.send_sems = send_sems
        self.pending = []

    def send(self, cond, src, dst, recv_sem, sp, tp):
        sem = self.send_sems.at[len(self.pending)]

        def make():
            return pltpu.make_async_remote_copy(
                src_ref=src,
                dst_ref=dst,
                send_sem=sem,
                recv_sem=recv_sem,
                device_id={"sp": sp, "tp": tp},
                device_id_type=pl.DeviceIdType.MESH,
            )

        self.pending.append((cond, make))
        when(cond, lambda: make().start())

    def arrive(self, dst, recv_sem, sp, tp):
        pltpu.make_async_remote_copy(
            src_ref=dst,
            dst_ref=dst,
            send_sem=self.send_sems.at[0],
            recv_sem=recv_sem,
            device_id={"sp": sp, "tp": tp},
            device_id_type=pl.DeviceIdType.MESH,
        ).wait_recv()

    def drain(self):
        for cond, make in self.pending:
            when(cond, lambda: make().wait_send())


def when(cond, body):
    if cond is True:
        body()
    else:
        pl.when(cond)(body)


def step_kernel(
    shape, x_ref, gain_ref, bits_ref, w_ref, query_ref, seg_ref, cot_ref,
    att_ref, gq_ref, ga_ref, gw_ref, gg_ref,
    wfull, hall, mask, inv, squares, dots, kvp, kvr, kvh, rim, rimx, rimo, rimr, own_grad, dkvall,
    own32, xsend, xr, zs, zru, zrd, ups, gains, probs, grads,
    send_sems, w_sem, w_recv, h_recv, sq_recv, dot_recv, kv_recv, halo_recv, rimx_recv, rim_recv, dkv_recv, dkc_recv,
    x_recv, up_recv, down_recv, gain_recv,
):
    S, T, X, Z, rows, F, WR, halo = shape
    R = T * rows
    places = S * T
    sp, tp = lax.axis_index("sp"), lax.axis_index("tp")
    c = sp % 2
    x = sp // 2 % X
    z = sp // (2 * X)
    place = tp * S + sp
    at = lambda zz, xx, cc: (zz * X + xx) * 2 + cc
    mate = at(z, x, 1 - c)
    links = Links(send_sems)
    order = [g for pair in zip(range(Z // 2), range(Z - 1, Z // 2 - 1, -1)) for g in pair]
    chunks = WR // 16
    cut = lambda k: pl.ds(k * 16, 16)
    tile = min(512, F)
    strip = 16
    lanes = F // 128

    fetch = pltpu.make_async_copy(w_ref, wfull.at[sp], w_sem)
    fetch.start()
    fetch.wait()

    def move_weight(cond, block, k, to):
        part = wfull.at[block, cut(k)]
        links.send(cond, part, part, w_recv.at[block, k], to, tp)

    def await_weight(cond, block, k):
        when(cond, lambda: links.arrive(wfull.at[block, cut(k)], w_recv.at[block, k], mate, tp))

    def own_up(cond):
        for k in range(chunks):
            move_weight(cond & (z < Z - 1), sp, k, at(z + 1, x, c))

    def own_down(cond):
        for k in range(chunks):
            move_weight(cond & (z > 0), sp, k, at(z - 1, x, c))

    def last_before(g, side):
        ahead = [b for b in order[: order.index(g)] if side(b, g)]
        return ahead[-1] if ahead else None

    up_after = {g: last_before(g, lambda b, a: b < a) for g in range(Z)}
    down_after = {g: last_before(g, lambda b, a: b > a) for g in range(Z)}
    for g in range(Z):
        if up_after[g] is None:
            own_up(z == g)
        if down_after[g] is None:
            own_down(z == g)
    for k in range(chunks):
        for j in range(1, X):
            move_weight(True, sp, k, at(z, (x + j) % X, c))
        move_weight(True, sp, k, mate)

    def weight_in(g, k):
        block = at(g, x, c)
        away = z != g
        await_weight(away, block, k)
        move_weight((z > g) & (z < Z - 1), block, k, at(z + 1, x, c))
        move_weight((z < g) & (z > 0), block, k, at(z - 1, x, c))
        for j in range(1, X):
            move_weight(away, block, k, at(z, (x + j) % X, c))
        move_weight(away, block, k, mate)
        if k == chunks - 1:
            for own in range(Z):
                if up_after[own] == g:
                    own_up(z == own)
                if down_after[own] == g:
                    own_down(z == own)

    def weight_x(g, k):
        for j in range(1, X):
            block = at(g, (x + j) % X, c)
            await_weight(True, block, k)
            move_weight(True, block, k, mate)

    def project(g):
        for k in range(chunks):
            for j in range(X):
                await_weight(True, at(g, j, 1 - c), k)
        weight = wfull[g * 2 * X : (g + 1) * 2 * X].reshape(2 * X * WR, F)
        part = lax.dot_general(hall[c], weight, NT, preferred_element_type=F32)
        for t in range(T):
            kvp[g, t] = part[t * rows : (t + 1) * rows]
        for k in range(1, T):
            to = (tp + k) % T
            links.send(True, kvp.at[g, to], kvr.at[g, tp], kv_recv.at[g, tp], sp, to)

    def square_rows(i, _):
        r = pl.ds(pl.multiple_of(i * strip, strip), strip)
        wide = x_ref[r, :].astype(F32)
        wide = wide * wide
        total = wide[:, :128]
        for k in range(1, lanes):
            total = total + wide[:, k * 128 : (k + 1) * 128]
        squares[tp, r, :] = total
        return 0

    lax.fori_loop(0, R // strip, square_rows, 0)
    for k in range(1, T):
        links.send(True, squares.at[tp], squares.at[tp], sq_recv.at[tp], sp, (tp + k) % T)
    early = chunks // 2
    for k in range(early):
        weight_in(order[0], k)

    words = min(128, F // 8)
    lane = lax.broadcasted_iota(jnp.int32, (words, words * 8), 1)
    expand = (lane // 8 == lax.broadcasted_iota(jnp.int32, (words, words * 8), 0)).astype(F32).astype(BF16)
    shifts = lax.broadcasted_iota(jnp.int32, (rows, words * 8), 1) % 8
    for w in range(F // 8 // words):
        def unpack(i, _):
            r = pl.ds(pl.multiple_of(i * rows, rows), rows)
            word = bits_ref[r, w * words : (w + 1) * words].astype(F32).astype(BF16)
            wide = jnp.dot(word, expand, preferred_element_type=F32).astype(jnp.int32)
            flag = jnp.bitwise_and(jnp.right_shift(wide, shifts), 1)
            mask[r, w * words * 8 : (w + 1) * words * 8] = flag.astype(F32).astype(BF16)
            return 0
        lax.fori_loop(0, T, unpack, 0)

    for k in range(1, T):
        links.arrive(squares.at[(tp + k) % T], sq_recv.at[(tp + k) % T], sp, (tp + k) % T)

    def norm_rows(i, _):
        r = pl.ds(pl.multiple_of(i * strip, strip), strip)
        total = squares[0, r, :]
        for t in range(1, T):
            total = total + squares[t, r, :]
        inv_rms = lax.rsqrt(jnp.sum(total, axis=1, keepdims=True) / D + EPS)
        inv[r, :] = jnp.broadcast_to(inv_rms, (strip, 128))
        wide = x_ref[r, :].astype(F32) * inv_rms * gain_ref[...].astype(F32)
        hall[c, r, :] = (wide * (mask[r, :].astype(F32) * DROP)).astype(BF16)
        return 0

    lax.fori_loop(0, R // strip, norm_rows, 0)
    for k in range(early, chunks):
        weight_in(order[0], k)
    links.send(True, hall.at[c], hall.at[c], h_recv, mate, tp)

    zero = lambda ref: (lambda: ref.__setitem__(Ellipsis, jnp.zeros(ref.shape, ref.dtype)))
    for slot in range(halo):
        pl.when(place + slot < halo)(zero(kvh.at[slot]))
    half = halo // 2
    for g in range(KVH):
        pl.when(c == 0)(zero(rimx.at[g, 0]))
        pl.when(c == 1)(zero(rimx.at[g, half]))
    keys = rows * (halo + 1)
    seg_rows = []
    for j in range(halo + 1):
        back = place - (halo - j)
        row = seg_ref[pl.ds(jnp.maximum(back, 0), 1), :]
        seg_rows.append(jnp.where(back >= 0, row, -1))
    seg_keys = jnp.concatenate(seg_rows, axis=1)
    seg_query = jnp.transpose(jnp.broadcast_to(seg_rows[halo].astype(F32), (rows, rows)))[:, :1]
    position = lax.broadcasted_iota(jnp.int32, (rows, keys), 0) + halo * rows
    other = lax.broadcasted_iota(jnp.int32, (rows, keys), 1)
    bias = jnp.where((other <= position) & (seg_query == seg_keys.astype(F32)), 0.0, MASKED_SCORE)

    def sum_pairs(g):
        total = kvp[g, tp]
        for k in range(1, T):
            other = (tp + k) % T
            links.arrive(kvr.at[g, other], kv_recv.at[g, other], sp, other)
            total = total + kvr[g, other]
        kvh[halo, g] = total.astype(BF16)
        for d in range(1, half + 1):
            to = place + 2 * d
            links.send(to < places, kvh.at[halo, g], kvh.at[halo - 2 * d, g], halo_recv.at[halo - 2 * d, g], to % S, to // S % T)
        links.send(c == 0, kvh.at[halo, g], kvh.at[halo - 1, g], halo_recv.at[halo - 1, g], mate, tp)

    def share_pairs(g):
        for d in range(1, half + 1):
            slot = halo - 2 * d
            here = place >= 2 * d
            when(here, lambda: links.arrive(kvh.at[slot, g], halo_recv.at[slot, g], mate, tp))
            links.send(here & (c == 1), kvh.at[slot, g], kvh.at[slot + 1, g], halo_recv.at[slot + 1, g], mate, tp)
            if slot > 0:
                links.send(here & (c == 0), kvh.at[slot, g], kvh.at[slot - 1, g], halo_recv.at[slot - 1, g], mate, tp)

    def await_pairs(g):
        for slot in range(1, halo, 2):
            when(place + slot >= halo, lambda: links.arrive(kvh.at[slot, g], halo_recv.at[slot, g], mate, tp))

    def attend(g, part):
        heads = GROUP // 2

        def head(i, _):
            n = part * heads + i
            pair = kvh[:, g].reshape(keys, KV)
            key_part, value_part = pair[:, :HD], pair[:, HD:]
            columns = pl.ds(pl.multiple_of((g * GROUP + n) * HD, HD), HD)
            below = pl.ds(pl.multiple_of(n * rows, rows), rows)
            query, grad = query_ref[:, columns], cot_ref[:, columns]
            scores = lax.dot_general(query, key_part, NT, preferred_element_type=F32) * SCALE
            scores = jnp.where(bias == 0.0, scores, MASKED_SCORE)
            weights = jnp.exp(scores - jnp.max(scores, axis=1, keepdims=True))
            prob = weights / jnp.sum(weights, axis=1, keepdims=True)
            low = prob.astype(BF16)
            att_ref[:, columns] = jnp.dot(low, value_part, preferred_element_type=F32).astype(BF16)
            grad_prob = lax.dot_general(grad, value_part, NT, preferred_element_type=F32)
            inner = jnp.sum(prob * grad_prob, axis=1, keepdims=True)
            grad_score = (prob * (grad_prob - inner)).astype(BF16)
            gq_ref[:, columns] = (jnp.dot(grad_score, key_part, preferred_element_type=F32) * SCALE).astype(BF16)
            probs[below, :] = low
            grads[below, :] = grad_score
            return 0

        lax.fori_loop(0, heads, head, 0, unroll=UNROLL)
        if part == 0:
            return
        column = lambda ref, n: ref[:, (g * GROUP + n) * HD : (g * GROUP + n + 1) * HD]
        queries = jnp.concatenate([column(query_ref, n) for n in range(GROUP)], axis=0)
        cots = jnp.concatenate([column(cot_ref, n) for n in range(GROUP)], axis=0)
        grad_key = lax.dot_general(grads[...], queries, TN, preferred_element_type=F32) * SCALE
        grad_value = lax.dot_general(probs[...], cots, TN, preferred_element_type=F32)
        for j in range(halo):
            r = slice(j * rows, (j + 1) * rows)
            rim[g, j, :, :HD] = grad_key[r]
            rim[g, j, :, HD:] = grad_value[r]
        own_grad[g, :, :HD] = grad_key[halo * rows :]
        own_grad[g, :, HD:] = grad_value[halo * rows :]
        for j in range(1, halo, 2):
            low, high = (j - 1) // 2, (j + 1) // 2
            links.send(c == 0, rim.at[g, j], rimx.at[g, low], rimx_recv.at[g, low], mate, tp)
            links.send(c == 1, rim.at[g, j], rimx.at[g, high], rimx_recv.at[g, high], mate, tp)

    def rim_out(g):
        for i in range(half + 1):
            cond = True if 0 < i < half else ((c == 1) if i == 0 else (c == 0))
            when(cond, lambda: links.arrive(rimx.at[g, i], rimx_recv.at[g, i], mate, tp))
        for d in range(1, half + 1):
            slot = halo - 2 * d
            rimo[g, d - 1] = (rim[g, slot] + rimx[g, slot // 2]).astype(BF16)
            to = place - 2 * d
            links.send(to >= 0, rimo.at[g, d - 1], rimr.at[g, d - 1], rim_recv.at[g, d - 1], (to + places) % S, (to + places) // S % T)
        own_grad[g] = own_grad[g] + rimx[g, half]

    def rim_in(g):
        for d in range(1, half + 1):
            def add():
                links.arrive(rimr.at[g, d - 1], rim_recv.at[g, d - 1], mate, tp)
                own_grad[g] = own_grad[g] + rimr[g, d - 1].astype(F32)
            pl.when(place + 2 * d < places)(add)
        dkvall[g, c, tp] = own_grad[g].astype(BF16)
        mine = dkvall.at[g, c, tp]
        for k in range(1, T):
            links.send(True, mine, mine, dkv_recv.at[g, tp], sp, (tp + k) % T)
        links.send(True, mine, mine, dkc_recv.at[g, tp], mate, tp)

    def pair_grads(g):
        for k in range(1, T):
            other = (tp + k) % T
            part = dkvall.at[g, c, other]
            links.arrive(part, dkv_recv.at[g, other], sp, other)
            links.send(True, part, part, dkc_recv.at[g, other], mate, tp)

    def weight_grad(g):
        for t in range(T):
            links.arrive(dkvall.at[g, 1 - c, t], dkc_recv.at[g, t], mate, tp)
        if g == order[0]:
            links.arrive(hall.at[1 - c], h_recv, mate, tp)
        turned = jnp.transpose(dkvall[g].reshape(2 * R, KV).astype(F32))
        rest = turned.reshape(X, 2, WR, 2 * R)
        rest = jnp.where(c == 0, rest[:, 0], rest[:, 1])
        picked = []
        for k in range(X):
            piece = rest[k]
            for j in range(X):
                piece = jnp.where((x + k) % X == j, rest[j], piece)
            picked.append(piece)
        left = jnp.concatenate(picked, axis=0).astype(BF16)

        def outer(i, _):
            columns = pl.ds(pl.multiple_of(i * tile, tile), tile)
            right = hall[:, :, columns].reshape(2 * R, tile)
            part = jnp.dot(left, right, preferred_element_type=F32)
            own32[g, :, columns] = part[:WR]
            for k in range(1, X):
                xsend[g, k - 1, :, columns] = part[k * WR : (k + 1) * WR].astype(BF16)
            return 0

        lax.fori_loop(0, F // tile, outer, 0)
        for q in range(chunks):
            for k in range(1, X):
                links.send(True, xsend.at[g, k - 1, cut(q)], xr.at[g, k - 1, cut(q)], x_recv.at[g, k - 1, q], at(z, (x + k) % X, c), tp)

    def fold(g, k, extra, out):
        def body(i, _):
            columns = pl.ds(pl.multiple_of(i * tile, tile), tile)
            value = own32[g, cut(k), columns]
            for ref in extra:
                value = value + ref[cut(k), columns].astype(F32)
            out(columns, value)
            return 0
        lax.fori_loop(0, F // tile, body, 0)

    def rows_out(g, k):
        for j in range(1, X):
            links.arrive(xr.at[g, j - 1, cut(k)], x_recv.at[g, j - 1, k], mate, tp)
        parts = [xr.at[g, j - 1] for j in range(1, X)]

        def send_low(columns, value):
            zs[g, cut(k), columns] = value.astype(BF16)

        def keep(columns, value):
            own32[g, cut(k), columns] = value

        def incoming(ref, sem):
            links.arrive(ref.at[g, cut(k)], sem.at[g, k], mate, tp)
            fold(g, k, parts + [ref.at[g]], send_low)

        if g > 0:
            pl.when(z == 0)(lambda: fold(g, k, parts, send_low))
            pl.when((z < g) & (z > 0))(lambda: incoming(zru, up_recv))
        if g < Z - 1:
            pl.when(z == Z - 1)(lambda: fold(g, k, parts, send_low))
            pl.when((z > g) & (z < Z - 1))(lambda: incoming(zrd, down_recv))
        pl.when(z == g)(lambda: fold(g, k, parts, keep))
        links.send(z < g, zs.at[g, cut(k)], zru.at[g, cut(k)], up_recv.at[g, k], at(z + 1, x, c), tp)
        links.send(z > g, zs.at[g, cut(k)], zrd.at[g, cut(k)], down_recv.at[g, k], at(z - 1, x, c), tp)

    first, second, third, fourth = order
    for k in range(chunks):
        weight_in(second, k)
        weight_x(first, k)
    project(first)
    for k in range(chunks):
        weight_in(third, k)
        weight_x(second, k)
        if k == 0:
            sum_pairs(first)
        if k == chunks - 1:
            share_pairs(first)
    project(second)
    await_pairs(first)
    attend(first, 0)
    sum_pairs(second)
    for k in range(chunks // 2):
        weight_in(fourth, k)
        weight_x(third, k)
    attend(first, 1)
    share_pairs(second)
    for k in range(chunks // 2, chunks):
        weight_in(fourth, k)
        weight_x(third, k)
    rim_out(first)
    project(third)
    await_pairs(second)
    attend(second, 0)
    sum_pairs(third)
    for k in range(chunks // 2):
        weight_x(fourth, k)
    rim_in(first)
    attend(second, 1)
    share_pairs(third)
    for k in range(chunks // 2, chunks):
        weight_x(fourth, k)
    pair_grads(first)
    rim_out(second)
    project(fourth)
    await_pairs(third)
    attend(third, 0)
    weight_grad(first)
    rim_in(second)
    sum_pairs(fourth)
    attend(third, 1)
    share_pairs(fourth)
    pair_grads(second)
    rim_out(third)
    await_pairs(fourth)
    attend(fourth, 0)
    weight_grad(second)
    rim_in(third)
    attend(fourth, 1)
    pair_grads(third)
    rim_out(fourth)
    for k in range(chunks):
        rows_out(first, k)
    weight_grad(third)
    rim_in(fourth)
    pair_grads(fourth)
    weight_grad(fourth)

    dkv_mine = jnp.concatenate([dkvall[g, c].reshape(R, KV) for g in range(KVH)], axis=1)
    dots[tp] = jnp.zeros((R, 128), F32)
    inv_column = inv[:, :1]

    def hidden(i, _):
        columns = pl.ds(pl.multiple_of(i * tile, tile), tile)
        weight = wfull[:, :, columns].reshape(S * WR, tile)
        scaled = jnp.dot(dkv_mine, weight, preferred_element_type=F32) * (mask[:, columns].astype(F32) * DROP)
        wide = x_ref[:, columns].astype(F32)
        gains[0, :, columns] = jnp.sum(scaled * wide * inv_column, axis=0, keepdims=True)
        upstream = scaled * gain_ref[:, columns].astype(F32)
        ups[:, columns] = upstream
        upstream = upstream * wide
        total = upstream[:, :128]
        for k in range(1, tile // 128):
            total = total + upstream[:, k * 128 : (k + 1) * 128]
        dots[tp] = dots[tp] + total
        return 0

    lax.fori_loop(0, F // tile, hidden, 0)
    for k in range(1, T):
        links.send(True, dots.at[tp], dots.at[tp], dot_recv.at[tp], sp, (tp + k) % T)
    links.send(True, gains.at[0], gains.at[1], gain_recv.at[1], mate, tp)
    for k in range(chunks):
        rows_out(second, k)
    links.arrive(gains.at[1], gain_recv.at[1], mate, tp)
    gains[2] = gains[0] + gains[1]
    for k in range(1, X):
        links.send(True, gains.at[2], gains.at[2 + k], gain_recv.at[2 + k], at(z, (x + k) % X, c), tp)
    for k in range(1, T):
        links.arrive(dots.at[(tp + k) % T], dot_recv.at[(tp + k) % T], sp, (tp + k) % T)

    def finish_rows(i, _):
        r = pl.ds(pl.multiple_of(i * strip, strip), strip)
        total = dots[0, r, :]
        for t in range(1, T):
            total = total + dots[t, r, :]
        row_dot = jnp.sum(total, axis=1, keepdims=True)
        scale = inv[r, :1]
        ga_ref[r, :] = (
            scale * ups[r, :] - x_ref[r, :].astype(F32) * ((scale * scale * scale) * row_dot / D)
        ).astype(BF16)
        return 0

    lax.fori_loop(0, R // strip, finish_rows, 0)
    for k in range(chunks):
        rows_out(third, k)
    for k in range(chunks):
        rows_out(fourth, k)
    total = gains[2]
    for k in range(1, X):
        links.arrive(gains.at[2 + k], gain_recv.at[2 + k], mate, tp)
        total = total + gains[2 + k]
    gains[2 + X] = total
    for k in range(1, Z):
        links.send(True, gains.at[2 + X], gains.at[2 + X + k], gain_recv.at[2 + X + k], at((z + k) % Z, x, c), tp)
    norm = (places * rows) ** (-0.5)

    for k in range(chunks):
        def result(columns, value):
            gw_ref[cut(k), columns] = value * norm

        pl.when(z > 0)(lambda: links.arrive(zru.at[z, cut(k)], up_recv.at[z, k], mate, tp))
        pl.when(z < Z - 1)(lambda: links.arrive(zrd.at[z, cut(k)], down_recv.at[z, k], mate, tp))
        pl.when(z == 0)(lambda: fold(z, k, [zrd.at[z]], result))
        pl.when(z == Z - 1)(lambda: fold(z, k, [zru.at[z]], result))
        pl.when((z > 0) & (z < Z - 1))(lambda: fold(z, k, [zru.at[z], zrd.at[z]], result))
    for k in range(1, Z):
        links.arrive(gains.at[2 + X + k], gain_recv.at[2 + X + k], mate, tp)
        total = total + gains[2 + X + k]
    gg_ref[...] = total * norm
    links.drain()


def on_device(activations, norm_gain, keep_bits, key_value_weight, queries, segment, cotangent):
    S, T = lax.axis_size("sp"), lax.axis_size("tp")
    blocks, rows, F = activations.shape
    WR = key_value_weight.shape[0]
    Z = KVH
    X = S // (2 * Z)
    R = blocks * rows
    halo = 2 * -(-(DOC - 1) // (2 * rows))
    keys = rows * (halo + 1)
    shape = (S, T, X, Z, rows, F, WR, halo)
    vmem = pl.BlockSpec(memory_space=pltpu.VMEM)
    dma = pltpu.SemaphoreType.DMA
    wide = queries.shape[-1]
    out = pl.pallas_call(
        functools.partial(step_kernel, shape),
        in_specs=[vmem, vmem, vmem, pl.BlockSpec(memory_space=pl.ANY), vmem, vmem, vmem],
        out_specs=[vmem] * 5,
        out_shape=[
            jax.ShapeDtypeStruct((rows, wide), BF16),
            jax.ShapeDtypeStruct((rows, wide), BF16),
            jax.ShapeDtypeStruct((R, F), BF16),
            jax.ShapeDtypeStruct((WR, F), F32),
            jax.ShapeDtypeStruct((1, F), F32),
        ],
        scratch_shapes=[
            pltpu.VMEM((S, WR, F), BF16),
            pltpu.VMEM((2, R, F), BF16),
            pltpu.VMEM((R, F), BF16),
            pltpu.VMEM((R, 128), F32),
            pltpu.VMEM((T, R, 128), F32),
            pltpu.VMEM((T, R, 128), F32),
            pltpu.VMEM((KVH, T, rows, KV), F32),
            pltpu.VMEM((KVH, T, rows, KV), F32),
            pltpu.VMEM((halo + 1, KVH, rows, KV), BF16),
            pltpu.VMEM((KVH, halo, rows, KV), F32),
            pltpu.VMEM((KVH, halo // 2 + 1, rows, KV), F32),
            pltpu.VMEM((KVH, halo // 2, rows, KV), BF16),
            pltpu.VMEM((KVH, halo // 2, rows, KV), BF16),
            pltpu.VMEM((KVH, rows, KV), F32),
            pltpu.VMEM((KVH, 2, T, rows, KV), BF16),
            pltpu.VMEM((Z, WR, F), F32),
            pltpu.VMEM((Z, X - 1, WR, F), BF16),
            pltpu.VMEM((Z, X - 1, WR, F), BF16),
            pltpu.VMEM((Z, WR, F), BF16),
            pltpu.VMEM((Z, WR, F), BF16),
            pltpu.VMEM((Z, WR, F), BF16),
            pltpu.VMEM((R, F), F32),
            pltpu.VMEM((2 + X + Z, 1, F), F32),
            pltpu.VMEM((GROUP * rows, keys), BF16),
            pltpu.VMEM((GROUP * rows, keys), BF16),
            dma((500,)),
            dma,
            dma((S, WR // 16)),
            dma,
            dma((T,)),
            dma((T,)),
            dma((KVH, T)),
            dma((halo, KVH)),
            dma((KVH, halo // 2 + 1)),
            dma((KVH, halo // 2)),
            dma((KVH, T)),
            dma((KVH, T)),
            dma((Z, X, WR // 16)),
            dma((Z, WR // 16)),
            dma((Z, WR // 16)),
            dma((2 + X + Z,)),
        ],
        compiler_params=pltpu.CompilerParams(has_side_effects=True, vmem_limit_bytes=63 * 2**20),
    )(
        activations.reshape(R, F),
        norm_gain.reshape(1, F),
        keep_bits.reshape(R, F // 8),
        key_value_weight,
        queries[0],
        segment.reshape(S * T, rows),
        cotangent[0],
    )
    attended, grad_queries, grad_activations, grad_weight, grad_gain = out
    return (
        attended[None],
        grad_queries[None],
        grad_activations.reshape(activations.shape),
        grad_weight,
        grad_gain.reshape(F),
    )


def solution(mesh):
    return jax.shard_map(
        on_device,
        mesh=mesh,
        in_specs=(
            P(None, "sp", "tp"),
            P("tp"),
            P(None, "sp", "tp"),
            P("sp", "tp"),
            P("tp", "sp", None),
            P(),
            P("tp", "sp", None),
        ),
        out_specs=(
            P("tp", "sp", None),
            P("tp", "sp", None),
            P(None, "sp", "tp"),
            P("sp", "tp"),
            P("tp"),
        ),
        check_vma=False,
    )
```

time: 269 us -> 210 us (0.78); the launches traced: 264 us -> 208 us
  Pallas kernels: 255 us -> 199 us
    pallas_call x1, Pallas kernels: 255 us -> 199 us  [on_device(): pl.pallas_call(functools.partial(step_kernel, shape), in_specs=[vmem, vme...]
where the time goes in v1:
time: 210 us; the launch traced here: 208 us
  Pallas kernels  199 us (95%)
  local copies, waits for them, and re-layouts  8.27 us (4%)
    pallas_call x1, Pallas kernels, on_device(): pl.pallas_call(functools.partial(step_kernel, shape), in_specs=[vmem, vme...  199 us
    unnamed x13, local copies, waits for them, and re-layouts  6.95 us

profile of v1, /device:TPU:12, one launch (start us, length us, event | category | flops | bytes accessed | tf_op | source)
XLA Modules:
  0.0 208.4 jit_solution(12465134694818819175)
XLA Ops:
  0.6 1.3 reshape.29.gain_ref
  1.9 199.5 %shard_map.110 = (bf16[128,4096]{1,0:T(8,128)(2,1)}, bf16[128,4096]{1,0:T(8,128)(2,1)}, bf16[256,4096]{1,0:T(8,128)(2,1)}, f32[64,4096]{1,0:T(8,128)}, f32[1,4096]{1,0:T(1,128)}) custom-call(bf16[256,4096]{1,0:T(8,128)(2,1)} %bitcast.9, bf16[1,4096]{1,0:T(2,128)(2,1)} %reshape.29.gain_ref, s32[256,512]{1,0:T(8,128)} %bitcast.15, bf16[64,4096]{1,0:T(8,128)(2,1)} %w_ref.1, ...), custom_call_target="tpu_custom_call" | custom-call | tf_op jit(solution)/shard_map/pallas_call | solution.py:549
  201.4 0.0 copy-start.2
  201.4 0.0 copy-start
  201.4 2.4 %copy.17 = bf16[1,128,4096]{2,1,0:T(8,128)(2,1)} copy(bf16[1,128,4096]{2,1,0:T(8,128)(2,1)} %bitcast.14) | data formatting | bytes 2097152
  203.9 0.0 copy-done.2
  203.9 1.0 copy.18
  204.8 0.0 copy-done
  204.8 0.0 copy-start.1
  204.9 1.3 copy.19
  206.2 0.6 copy-done.1
  206.8 0.0 copy-start.3
  206.8 1.0 copy.20
  207.8 0.0 copy-done.3
  207.8 0.6 copy.21
Async XLA Ops:
  201.4 2.5 %copy-start.2 = (bf16[128,4096]{1,0:T(8,128)(2,1)S(1)}, bf16[128,4096]{1,0:T(8,128)(2,1)}, u32[]{:S(2)}) copy-start(bf16[128,4096]{1,0:T(8,128)(2,1)} %get-tuple-element.11) | copy-start | bytes 3145732
  201.4 3.4 %copy-start = (bf16[256,4096]{1,0:T(8,128)(2,1)S(1)}, bf16[256,4096]{1,0:T(8,128)(2,1)}, u32[]{:S(2)}) copy-start(bf16[256,4096]{1,0:T(8,128)(2,1)} %get-tuple-element.12) | copy-start | bytes 6291460
  204.8 2.0 copy-start.1
  206.8 1.0 copy-start.3

commit v2 on v1

--- a/solution.py
+++ b/solution.py
@@ -24,6 +24,7 @@
 BF16 = jnp.bfloat16
 NT = (((1,), (1,)), ((), ()))
 UNROLL = 2
+LOG2E = 1.4426950408889634
 TN = (((0,), (0,)), ((), ()))
 
 
@@ -71,12 +72,13 @@
 
 
 def step_kernel(
-    shape, x_ref, gain_ref, bits_ref, w_ref, query_ref, seg_ref, cot_ref,
-    att_ref, gq_ref, ga_ref, gw_ref, gg_ref,
+    shape, x_hbm, gain_ref, bits_hbm, w_ref, query_hbm, seg_ref, cot_hbm,
+    att_hbm, gq_hbm, ga_hbm, gw_hbm, gg_ref,
+    x_ref, bits_ref, query_ref, cot_ref, att_ref, gq_ref, ga_ref, gw_ref,
     wfull, hall, mask, inv, squares, dots, kvp, kvr, kvh, rim, rimx, rimo, rimr, own_grad, dkvall,
-    own32, xsend, xr, zs, zru, zrd, ups, gains, probs, grads,
-    send_sems, w_sem, w_recv, h_recv, sq_recv, dot_recv, kv_recv, halo_recv, rimx_recv, rim_recv, dkv_recv, dkc_recv,
-    x_recv, up_recv, down_recv, gain_recv,
+    own32, xsend, xr, zs, zr, ups, gains, probs, grads, bias,
+    send_sems, local_sems, w_recv, h_recv, sq_recv, dot_recv, kv_recv, halo_recv, rimx_recv, rim_recv, dkv_recv, dkc_recv,
+    x_recv, z_recv, gain_recv,
 ):
     S, T, X, Z, rows, F, WR, halo = shape
     R = T * rows
@@ -89,16 +91,54 @@
     at = lambda zz, xx, cc: (zz * X + xx) * 2 + cc
     mate = at(z, x, 1 - c)
     links = Links(send_sems)
-    order = [g for pair in zip(range(Z // 2), range(Z - 1, Z // 2 - 1, -1)) for g in pair]
+    order = [g for pair in zip(range(Z - 1, Z // 2 - 1, -1), range(Z // 2)) for g in pair]
     chunks = WR // 16
     cut = lambda k: pl.ds(k * 16, 16)
     tile = min(512, F)
     strip = 16
     lanes = F // 128
 
-    fetch = pltpu.make_async_copy(w_ref, wfull.at[sp], w_sem)
-    fetch.start()
-    fetch.wait()
+    inputs = [
+        pltpu.make_async_copy(w_ref, wfull.at[sp], local_sems.at[0]),
+        pltpu.make_async_copy(x_hbm, x_ref, local_sems.at[1]),
+        pltpu.make_async_copy(bits_hbm, bits_ref, local_sems.at[2]),
+        pltpu.make_async_copy(query_hbm, query_ref, local_sems.at[3]),
+        pltpu.make_async_copy(cot_hbm, cot_ref, local_sems.at[4]),
+    ]
+    for copy in inputs:
+        copy.start()
+    results = []
+
+    def put_out(src, dst):
+        copy = pltpu.make_async_copy(src, dst, local_sems.at[len(inputs) + len(results)])
+        copy.start()
+        results.append(copy)
+
+    half = halo // 2
+    barrier = pltpu.get_barrier_semaphore()
+
+    def greet(cond, to_sp, to_tp):
+        when(cond, lambda: pl.semaphore_signal(
+            barrier, inc=1, device_id={"sp": to_sp, "tp": to_tp}, device_id_type=pl.DeviceIdType.MESH
+        ))
+
+    for k in range(1, Z):
+        greet(True, at((z + k) % Z, x, c), tp)
+    for k in range(1, X):
+        greet(True, at(z, (x + k) % X, c), tp)
+    greet(True, mate, tp)
+    for k in range(1, T):
+        greet(True, sp, (tp + k) % T)
+    greeted = Z - 1 + X - 1 + 1 + T - 1
+    for d in range(1, half + 1):
+        for to in (place + 2 * d, place - 2 * d):
+            inside = (to >= 0) & (to < places)
+            greet(inside, (to + places) % S, (to + places) // S % T)
+            greeted = greeted + jnp.where(inside, 1, 0)
+    pl.semaphore_wait(barrier, greeted)
+    inputs[0].wait()
+
+    relayed, direct = order[:2], order[2:]
 
     def move_weight(cond, block, k, to):
         part = wfull.at[block, cut(k)]
@@ -107,45 +147,35 @@
     def await_weight(cond, block, k):
         when(cond, lambda: links.arrive(wfull.at[block, cut(k)], w_recv.at[block, k], mate, tp))
 
-    def own_up(cond):
+    for g in relayed:
         for k in range(chunks):
-            move_weight(cond & (z < Z - 1), sp, k, at(z + 1, x, c))
-
-    def own_down(cond):
-        for k in range(chunks):
-            move_weight(cond & (z > 0), sp, k, at(z - 1, x, c))
-
-    def last_before(g, side):
-        ahead = [b for b in order[: order.index(g)] if side(b, g)]
-        return ahead[-1] if ahead else None
-
-    up_after = {g: last_before(g, lambda b, a: b < a) for g in range(Z)}
-    down_after = {g: last_before(g, lambda b, a: b > a) for g in range(Z)}
-    for g in range(Z):
-        if up_after[g] is None:
-            own_up(z == g)
-        if down_after[g] is None:
-            own_down(z == g)
-    for k in range(chunks):
+            if g < Z - 1:
+                move_weight(z == g, sp, k, at(z + 1, x, c))
+            if g > 0:
+                move_weight(z == g, sp, k, at(z - 1, x, c))
+            for j in range(1, X):
+                move_weight(z == g, sp, k, at(z, (x + j) % X, c))
+    for k in range(chunks):
+        move_weight(True, sp, k, mate)
+
+    def weight_direct(g, k):
+        for d in range(Z - 1, 0, -1):
+            for to in (g - d, g + d):
+                if 0 <= to < Z:
+                    move_weight(z == g, sp, k, at(to, x, c))
         for j in range(1, X):
-            move_weight(True, sp, k, at(z, (x + j) % X, c))
-        move_weight(True, sp, k, mate)
-
-    def weight_in(g, k):
+            move_weight(z == g, sp, k, at(z, (x + j) % X, c))
+
+    def weight_in(g, k, relay=False):
         block = at(g, x, c)
         away = z != g
         await_weight(away, block, k)
-        move_weight((z > g) & (z < Z - 1), block, k, at(z + 1, x, c))
-        move_weight((z < g) & (z > 0), block, k, at(z - 1, x, c))
+        if relay:
+            move_weight((z > g) & (z < Z - 1), block, k, at(z + 1, x, c))
+            move_weight((z < g) & (z > 0), block, k, at(z - 1, x, c))
         for j in range(1, X):
             move_weight(away, block, k, at(z, (x + j) % X, c))
         move_weight(away, block, k, mate)
-        if k == chunks - 1:
-            for own in range(Z):
-                if up_after[own] == g:
-                    own_up(z == own)
-                if down_after[own] == g:
-                    own_down(z == own)
 
     def weight_x(g, k):
         for j in range(1, X):
@@ -175,13 +205,14 @@
         squares[tp, r, :] = total
         return 0
 
+    inputs[1].wait()
     lax.fori_loop(0, R // strip, square_rows, 0)
     for k in range(1, T):
         links.send(True, squares.at[tp], squares.at[tp], sq_recv.at[tp], sp, (tp + k) % T)
-    early = chunks // 2
-    for k in range(early):
-        weight_in(order[0], k)
-
+    near = jnp.where(z < Z // 2, relayed[1], relayed[0])
+    far = jnp.where(z < Z // 2, relayed[0], relayed[1])
+    weight_in(near, 0, True)
+    inputs[2].wait()
     words = min(128, F // 8)
     lane = lax.broadcasted_iota(jnp.int32, (words, words * 8), 1)
     expand = (lane // 8 == lax.broadcasted_iota(jnp.int32, (words, words * 8), 0)).astype(F32).astype(BF16)
@@ -195,9 +226,10 @@
             mask[r, w * words * 8 : (w + 1) * words * 8] = flag.astype(F32).astype(BF16)
             return 0
         lax.fori_loop(0, T, unpack, 0)
-
     for k in range(1, T):
         links.arrive(squares.at[(tp + k) % T], sq_recv.at[(tp + k) % T], sp, (tp + k) % T)
+    weight_in(near, 1, True)
+    weight_in(far, 0, True)
 
     def norm_rows(i, _):
         r = pl.ds(pl.multiple_of(i * strip, strip), strip)
@@ -211,14 +243,15 @@
         return 0
 
     lax.fori_loop(0, R // strip, norm_rows, 0)
-    for k in range(early, chunks):
-        weight_in(order[0], k)
+    for k in range(2, chunks):
+        weight_in(near, k, True)
+        weight_in(far, k - 1, True)
+    weight_in(far, chunks - 1, True)
     links.send(True, hall.at[c], hall.at[c], h_recv, mate, tp)
 
     zero = lambda ref: (lambda: ref.__setitem__(Ellipsis, jnp.zeros(ref.shape, ref.dtype)))
     for slot in range(halo):
         pl.when(place + slot < halo)(zero(kvh.at[slot]))
-    half = halo // 2
     for g in range(KVH):
         pl.when(c == 0)(zero(rimx.at[g, 0]))
         pl.when(c == 1)(zero(rimx.at[g, half]))
@@ -232,7 +265,7 @@
     seg_query = jnp.transpose(jnp.broadcast_to(seg_rows[halo].astype(F32), (rows, rows)))[:, :1]
     position = lax.broadcasted_iota(jnp.int32, (rows, keys), 0) + halo * rows
     other = lax.broadcasted_iota(jnp.int32, (rows, keys), 1)
-    bias = jnp.where((other <= position) & (seg_query == seg_keys.astype(F32)), 0.0, MASKED_SCORE)
+    bias[...] = jnp.where((other <= position) & (seg_query == seg_keys.astype(F32)), 0.0, MASKED_SCORE)
 
     def sum_pairs(g):
         total = kvp[g, tp]
@@ -269,10 +302,9 @@
             columns = pl.ds(pl.multiple_of((g * GROUP + n) * HD, HD), HD)
             below = pl.ds(pl.multiple_of(n * rows, rows), rows)
             query, grad = query_ref[:, columns], cot_ref[:, columns]
-            scores = lax.dot_general(query, key_part, NT, preferred_element_type=F32) * SCALE
-            scores = jnp.where(bias == 0.0, scores, MASKED_SCORE)
-            weights = jnp.exp(scores - jnp.max(scores, axis=1, keepdims=True))
-            prob = weights / jnp.sum(weights, axis=1, keepdims=True)
+            scores = lax.dot_general(query, key_part, NT, preferred_element_type=F32) * (SCALE * LOG2E) + bias[...]
+            weights = jnp.exp2(scores - jnp.max(scores, axis=1, keepdims=True))
+            prob = weights * (1.0 / jnp.sum(weights, axis=1, keepdims=True))
             low = prob.astype(BF16)
             att_ref[:, columns] = jnp.dot(low, value_part, preferred_element_type=F32).astype(BF16)
             grad_prob = lax.dot_general(grad, value_part, NT, preferred_element_type=F32)
@@ -286,6 +318,9 @@
         lax.fori_loop(0, heads, head, 0, unroll=UNROLL)
         if part == 0:
             return
+        wide = pl.ds(g * GROUP * HD, GROUP * HD)
+        put_out(att_ref.at[:, wide], att_hbm.at[:, wide])
+        put_out(gq_ref.at[:, wide], gq_hbm.at[:, wide])
         column = lambda ref, n: ref[:, (g * GROUP + n) * HD : (g * GROUP + n + 1) * HD]
         queries = jnp.concatenate([column(query_ref, n) for n in range(GROUP)], axis=0)
         cots = jnp.concatenate([column(cot_ref, n) for n in range(GROUP)], axis=0)
@@ -383,78 +418,75 @@
         def keep(columns, value):
             own32[g, cut(k), columns] = value
 
-        def incoming(ref, sem):
-            links.arrive(ref.at[g, cut(k)], sem.at[g, k], mate, tp)
-            fold(g, k, parts + [ref.at[g]], send_low)
-
-        if g > 0:
-            pl.when(z == 0)(lambda: fold(g, k, parts, send_low))
-            pl.when((z < g) & (z > 0))(lambda: incoming(zru, up_recv))
-        if g < Z - 1:
-            pl.when(z == Z - 1)(lambda: fold(g, k, parts, send_low))
-            pl.when((z > g) & (z < Z - 1))(lambda: incoming(zrd, down_recv))
         pl.when(z == g)(lambda: fold(g, k, parts, keep))
-        links.send(z < g, zs.at[g, cut(k)], zru.at[g, cut(k)], up_recv.at[g, k], at(z + 1, x, c), tp)
-        links.send(z > g, zs.at[g, cut(k)], zrd.at[g, cut(k)], down_recv.at[g, k], at(z - 1, x, c), tp)
+        pl.when(z != g)(lambda: fold(g, k, parts, send_low))
+        links.send(z != g, zs.at[g, cut(k)], zr.at[z, cut(k)], z_recv.at[z, k], at(g, x, c), tp)
 
     first, second, third, fourth = order
     for k in range(chunks):
-        weight_in(second, k)
+        weight_direct(third, k)
+        weight_direct(fourth, k)
+    inputs[3].wait()
+    inputs[4].wait()
+    for k in range(chunks):
         weight_x(first, k)
+        weight_x(second, k)
     project(first)
-    for k in range(chunks):
+    weight_in(third, 0)
+    weight_in(third, 1)
+    project(second)
+    for k in range(2, chunks):
         weight_in(third, k)
-        weight_x(second, k)
-        if k == 0:
-            sum_pairs(first)
-        if k == chunks - 1:
-            share_pairs(first)
-    project(second)
+        weight_x(third, k - 2)
+    weight_in(fourth, 0)
+    sum_pairs(first)
+    sum_pairs(second)
+    for k in range(1, max(chunks - 1, 2)):
+        weight_in(fourth, k)
+    for k in range(chunks - 2, chunks):
+        weight_x(third, k)
+    share_pairs(first)
     await_pairs(first)
     attend(first, 0)
-    sum_pairs(second)
-    for k in range(chunks // 2):
+    for k in range(max(chunks - 1, 2), chunks):
         weight_in(fourth, k)
-        weight_x(third, k)
+    for k in range(chunks - 1):
+        weight_x(fourth, k)
+    share_pairs(second)
     attend(first, 1)
-    share_pairs(second)
-    for k in range(chunks // 2, chunks):
-        weight_in(fourth, k)
-        weight_x(third, k)
+    weight_x(fourth, chunks - 1)
+    await_pairs(second)
     rim_out(first)
+    attend(second, 0)
     project(third)
-    await_pairs(second)
-    attend(second, 0)
-    sum_pairs(third)
-    for k in range(chunks // 2):
-        weight_x(fourth, k)
+    project(fourth)
     rim_in(first)
     attend(second, 1)
+    sum_pairs(third)
+    sum_pairs(fourth)
+    rim_out(second)
+    pair_grads(first)
+    weight_grad(first)
     share_pairs(third)
-    for k in range(chunks // 2, chunks):
-        weight_x(fourth, k)
-    pair_grads(first)
-    rim_out(second)
-    project(fourth)
     await_pairs(third)
     attend(third, 0)
-    weight_grad(first)
+    share_pairs(fourth)
     rim_in(second)
-    sum_pairs(fourth)
     attend(third, 1)
-    share_pairs(fourth)
     pair_grads(second)
-    rim_out(third)
+    weight_grad(second)
     await_pairs(fourth)
     attend(fourth, 0)
-    weight_grad(second)
+    rim_out(third)
+    for k in range(chunks):
+        rows_out(first, k)
+    attend(fourth, 1)
+    rim_out(fourth)
     rim_in(third)
-    attend(fourth, 1)
     pair_grads(third)
-    rim_out(fourth)
-    for k in range(chunks):
-        rows_out(first, k)
     weight_grad(third)
+    for k in range(chunks):
+        rows_out(second, k)
     rim_in(fourth)
     pair_grads(fourth)
     weight_grad(fourth)
@@ -482,12 +514,21 @@
     for k in range(1, T):
         links.send(True, dots.at[tp], dots.at[tp], dot_recv.at[tp], sp, (tp + k) % T)
     links.send(True, gains.at[0], gains.at[1], gain_recv.at[1], mate, tp)
-    for k in range(chunks):
-        rows_out(second, k)
     links.arrive(gains.at[1], gain_recv.at[1], mate, tp)
     gains[2] = gains[0] + gains[1]
+    for k in range(1, Z):
+        links.send(True, gains.at[2], gains.at[2 + k], gain_recv.at[2 + k], at((z + k) % Z, x, c), tp)
+    for k in range(chunks):
+        rows_out(third, k)
+    total = gains[2]
+    for k in range(1, Z):
+        links.arrive(gains.at[2 + k], gain_recv.at[2 + k], mate, tp)
+        total = total + gains[2 + k]
+    gains[2 + Z] = total
     for k in range(1, X):
-        links.send(True, gains.at[2], gains.at[2 + k], gain_recv.at[2 + k], at(z, (x + k) % X, c), tp)
+        links.send(True, gains.at[2 + Z], gains.at[2 + Z + k], gain_recv.at[2 + Z + k], at(z, (x + k) % X, c), tp)
+    for k in range(chunks):
+        rows_out(fourth, k)
     for k in range(1, T):
         links.arrive(dots.at[(tp + k) % T], dot_recv.at[(tp + k) % T], sp, (tp + k) % T)
 
@@ -504,33 +545,25 @@
         return 0
 
     lax.fori_loop(0, R // strip, finish_rows, 0)
-    for k in range(chunks):
-        rows_out(third, k)
-    for k in range(chunks):
-        rows_out(fourth, k)
-    total = gains[2]
-    for k in range(1, X):
-        links.arrive(gains.at[2 + k], gain_recv.at[2 + k], mate, tp)
-        total = total + gains[2 + k]
-    gains[2 + X] = total
-    for k in range(1, Z):
-        links.send(True, gains.at[2 + X], gains.at[2 + X + k], gain_recv.at[2 + X + k], at((z + k) % Z, x, c), tp)
+    put_out(ga_ref, ga_hbm)
     norm = (places * rows) ** (-0.5)
 
     for k in range(chunks):
         def result(columns, value):
             gw_ref[cut(k), columns] = value * norm
 
-        pl.when(z > 0)(lambda: links.arrive(zru.at[z, cut(k)], up_recv.at[z, k], mate, tp))
-        pl.when(z < Z - 1)(lambda: links.arrive(zrd.at[z, cut(k)], down_recv.at[z, k], mate, tp))
-        pl.when(z == 0)(lambda: fold(z, k, [zrd.at[z]], result))
-        pl.when(z == Z - 1)(lambda: fold(z, k, [zru.at[z]], result))
-        pl.when((z > 0) & (z < Z - 1))(lambda: fold(z, k, [zru.at[z], zrd.at[z]], result))
-    for k in range(1, Z):
-        links.arrive(gains.at[2 + X + k], gain_recv.at[2 + X + k], mate, tp)
-        total = total + gains[2 + X + k]
+        sources = [(z + j) % Z for j in range(1, Z)]
+        for source in sources:
+            links.arrive(zr.at[source, cut(k)], z_recv.at[source, k], mate, tp)
+        fold(z, k, [zr.at[source] for source in sources], result)
+        put_out(gw_ref.at[cut(k)], gw_hbm.at[cut(k)])
+    for k in range(1, X):
+        links.arrive(gains.at[2 + Z + k], gain_recv.at[2 + Z + k], mate, tp)
+        total = total + gains[2 + Z + k]
     gg_ref[...] = total * norm
     links.drain()
+    for copy in results:
+        copy.wait()
 
 
 def on_device(activations, norm_gain, keep_bits, key_value_weight, queries, segment, cotangent):
@@ -544,12 +577,13 @@
     keys = rows * (halo + 1)
     shape = (S, T, X, Z, rows, F, WR, halo)
     vmem = pl.BlockSpec(memory_space=pltpu.VMEM)
+    hbm = pl.BlockSpec(memory_space=pl.ANY)
     dma = pltpu.SemaphoreType.DMA
     wide = queries.shape[-1]
     out = pl.pallas_call(
         functools.partial(step_kernel, shape),
-        in_specs=[vmem, vmem, vmem, pl.BlockSpec(memory_space=pl.ANY), vmem, vmem, vmem],
-        out_specs=[vmem] * 5,
+        in_specs=[hbm, vmem, hbm, hbm, hbm, vmem, hbm],
+        out_specs=[hbm] * 4 + [vmem],
         out_shape=[
             jax.ShapeDtypeStruct((rows, wide), BF16),
             jax.ShapeDtypeStruct((rows, wide), BF16),
@@ -558,6 +592,14 @@
             jax.ShapeDtypeStruct((1, F), F32),
         ],
         scratch_shapes=[
+            pltpu.VMEM((R, F), BF16),
+            pltpu.VMEM((R, F // 8), jnp.int32),
+            pltpu.VMEM((rows, wide), BF16),
+            pltpu.VMEM((rows, wide), BF16),
+            pltpu.VMEM((rows, wide), BF16),
+            pltpu.VMEM((rows, wide), BF16),
+            pltpu.VMEM((R, F), BF16),
+            pltpu.VMEM((WR, F), F32),
             pltpu.VMEM((S, WR, F), BF16),
             pltpu.VMEM((2, R, F), BF16),
             pltpu.VMEM((R, F), BF16),
@@ -578,13 +620,13 @@
             pltpu.VMEM((Z, X - 1, WR, F), BF16),
             pltpu.VMEM((Z, WR, F), BF16),
             pltpu.VMEM((Z, WR, F), BF16),
-            pltpu.VMEM((Z, WR, F), BF16),
             pltpu.VMEM((R, F), F32),
             pltpu.VMEM((2 + X + Z, 1, F), F32),
             pltpu.VMEM((GROUP * rows, keys), BF16),
             pltpu.VMEM((GROUP * rows, keys), BF16),
+            pltpu.VMEM((rows, keys), F32),
             dma((500,)),
-            dma,
+            dma((32,)),
             dma((S, WR // 16)),
             dma,
             dma((T,)),
@@ -597,10 +639,9 @@
             dma((KVH, T)),
             dma((Z, X, WR // 16)),
             dma((Z, WR // 16)),
-            dma((Z, WR // 16)),
             dma((2 + X + Z,)),
         ],
-        compiler_params=pltpu.CompilerParams(has_side_effects=True, vmem_limit_bytes=63 * 2**20),
+        compiler_params=pltpu.CompilerParams(collective_id=0, has_side_effects=True, vmem_limit_bytes=63 * 2**20),
     )(
         activations.reshape(R, F),
         norm_gain.reshape(1, F),

time: 210 us -> 185 us (0.88)
  Pallas kernels: 199 us -> 174 us
    pallas_call x1, Pallas kernels: 199 us -> 174 us  [on_device(): pl.pallas_call(functools.partial(step_kernel, shape), in_specs=[hbm, vmem...]
where the time goes in v2:
time: 185 us; the launch traced here: 183 us
  Pallas kernels  174 us (94%)
  local copies, waits for them, and re-layouts  8.27 us (4%)
    pallas_call x1, Pallas kernels, on_device(): pl.pallas_call(functools.partial(step_kernel, shape), in_specs=[hbm, vmem...  174 us
    unnamed x13, local copies, waits for them, and re-layouts  6.95 us

profile of v2, /device:TPU:12, one launch (start us, length us, event | category | flops | bytes accessed | tf_op | source)
XLA Modules:
  0.0 183.4 jit_solution(142313821035391760)
XLA Ops:
  0.6 1.3 reshape.29.gain_ref
  1.9 174.5 %shard_map.110 = (bf16[128,4096]{1,0:T(8,128)(2,1)}, bf16[128,4096]{1,0:T(8,128)(2,1)}, bf16[256,4096]{1,0:T(8,128)(2,1)}, f32[64,4096]{1,0:T(8,128)}, f32[1,4096]{1,0:T(1,128)}) custom-call(bf16[256,4096]{1,0:T(8,128)(2,1)} %bitcast.9, bf16[1,4096]{1,0:T(2,128)(2,1)} %reshape.29.gain_ref, s32[256,512]{1,0:T(8,128)} %bitcast.15, bf16[64,4096]{1,0:T(8,128)(2,1)} %w_ref.1, ...), custom_call_target="tpu_custom_call" | custom-call | tf_op jit(solution)/shard_map/pallas_call | solution.py:583
  176.4 0.0 copy-start.2
  176.4 0.0 copy-start
  176.4 2.4 %copy.17 = bf16[1,128,4096]{2,1,0:T(8,128)(2,1)} copy(bf16[1,128,4096]{2,1,0:T(8,128)(2,1)} %bitcast.14) | data formatting | bytes 2097152
  178.9 0.0 copy-done.2
  178.9 1.0 copy.18
  179.9 0.0 copy-done
  179.9 0.0 copy-start.1
  179.9 1.3 copy.19
  181.2 0.6 copy-done.1
  181.8 0.0 copy-start.3
  181.8 1.0 copy.20
  182.8 0.0 copy-done.3
  182.8 0.6 copy.21
Async XLA Ops:
  176.4 2.5 %copy-start.2 = (bf16[128,4096]{1,0:T(8,128)(2,1)S(1)}, bf16[128,4096]{1,0:T(8,128)(2,1)}, u32[]{:S(2)}) copy-start(bf16[128,4096]{1,0:T(8,128)(2,1)} %get-tuple-element.11) | copy-start | bytes 3145732
  176.4 3.4 %copy-start = (bf16[256,4096]{1,0:T(8,128)(2,1)S(1)}, bf16[256,4096]{1,0:T(8,128)(2,1)}, u32[]{:S(2)}) copy-start(bf16[256,4096]{1,0:T(8,128)(2,1)} %get-tuple-element.12) | copy-start | bytes 6291460
  179.9 2.0 %copy-start.1 = (f32[64,4096]{1,0:T(8,128)S(1)}, f32[64,4096]{1,0:T(8,128)}, u32[]{:S(2)}) copy-start(f32[64,4096]{1,0:T(8,128)} %get-tuple-element.23) | copy-start | bytes 3145732
  181.8 1.0 copy-start.3

commit v3 on v2

--- a/solution.py
+++ b/solution.py
@@ -23,7 +23,8 @@
 F32 = jnp.float32
 BF16 = jnp.bfloat16
 NT = (((1,), (1,)), ((), ()))
-UNROLL = 2
+UNROLL = 1
+BATCH = 4
 LOG2E = 1.4426950408889634
 TN = (((0,), (0,)), ((), ()))
 
@@ -32,9 +33,11 @@
     def __init__(self, send_sems):
         self.send_sems = send_sems
         self.pending = []
-
-    def send(self, cond, src, dst, recv_sem, sp, tp):
-        sem = self.send_sems.at[len(self.pending)]
+        self.used = 0
+
+    def send(self, cond, src, dst, recv_sem, sp, tp, again=False):
+        self.used += not again
+        sem = self.send_sems.at[self.used - 1]
 
         def make():
             return pltpu.make_async_remote_copy(
@@ -76,9 +79,9 @@
     att_hbm, gq_hbm, ga_hbm, gw_hbm, gg_ref,
     x_ref, bits_ref, query_ref, cot_ref, att_ref, gq_ref, ga_ref, gw_ref,
     wfull, hall, mask, inv, squares, dots, kvp, kvr, kvh, rim, rimx, rimo, rimr, own_grad, dkvall,
-    own32, xsend, xr, zs, zr, ups, gains, probs, grads, bias,
+    own32, xsend, xr, zs, zr, za, ups, gains, probs, grads, bias, gain_row,
     send_sems, local_sems, w_recv, h_recv, sq_recv, dot_recv, kv_recv, halo_recv, rimx_recv, rim_recv, dkv_recv, dkc_recv,
-    x_recv, z_recv, gain_recv,
+    x_recv, z_recv, a_recv, gain_recv,
 ):
     S, T, X, Z, rows, F, WR, halo = shape
     R = T * rows
@@ -140,9 +143,9 @@
 
     relayed, direct = order[:2], order[2:]
 
-    def move_weight(cond, block, k, to):
+    def move_weight(cond, block, k, to, again=False):
         part = wfull.at[block, cut(k)]
-        links.send(cond, part, part, w_recv.at[block, k], to, tp)
+        links.send(cond, part, part, w_recv.at[block, k], to, tp, again)
 
     def await_weight(cond, block, k):
         when(cond, lambda: links.arrive(wfull.at[block, cut(k)], w_recv.at[block, k], mate, tp))
@@ -172,7 +175,7 @@
         await_weight(away, block, k)
         if relay:
             move_weight((z > g) & (z < Z - 1), block, k, at(z + 1, x, c))
-            move_weight((z < g) & (z > 0), block, k, at(z - 1, x, c))
+            move_weight((z < g) & (z > 0), block, k, at(z - 1, x, c), True)
         for j in range(1, X):
             move_weight(away, block, k, at(z, (x + j) % X, c))
         move_weight(away, block, k, mate)
@@ -206,6 +209,7 @@
         return 0
 
     inputs[1].wait()
+    gain_row[...] = gain_ref[...].astype(F32).reshape(1, F)
     lax.fori_loop(0, R // strip, square_rows, 0)
     for k in range(1, T):
         links.send(True, squares.at[tp], squares.at[tp], sq_recv.at[tp], sp, (tp + k) % T)
@@ -238,7 +242,7 @@
             total = total + squares[t, r, :]
         inv_rms = lax.rsqrt(jnp.sum(total, axis=1, keepdims=True) / D + EPS)
         inv[r, :] = jnp.broadcast_to(inv_rms, (strip, 128))
-        wide = x_ref[r, :].astype(F32) * inv_rms * gain_ref[...].astype(F32)
+        wide = x_ref[r, :].astype(F32) * inv_rms * gain_row[...]
         hall[c, r, :] = (wide * (mask[r, :].astype(F32) * DROP)).astype(BF16)
         return 0
 
@@ -286,7 +290,7 @@
             when(here, lambda: links.arrive(kvh.at[slot, g], halo_recv.at[slot, g], mate, tp))
             links.send(here & (c == 1), kvh.at[slot, g], kvh.at[slot + 1, g], halo_recv.at[slot + 1, g], mate, tp)
             if slot > 0:
-                links.send(here & (c == 0), kvh.at[slot, g], kvh.at[slot - 1, g], halo_recv.at[slot - 1, g], mate, tp)
+                links.send(here & (c == 0), kvh.at[slot, g], kvh.at[slot - 1, g], halo_recv.at[slot - 1, g], mate, tp, True)
 
     def await_pairs(g):
         for slot in range(1, halo, 2):
@@ -295,27 +299,35 @@
     def attend(g, part):
         heads = GROUP // 2
 
-        def head(i, _):
-            n = part * heads + i
-            pair = kvh[:, g].reshape(keys, KV)
-            key_part, value_part = pair[:, :HD], pair[:, HD:]
-            columns = pl.ds(pl.multiple_of((g * GROUP + n) * HD, HD), HD)
-            below = pl.ds(pl.multiple_of(n * rows, rows), rows)
-            query, grad = query_ref[:, columns], cot_ref[:, columns]
-            scores = lax.dot_general(query, key_part, NT, preferred_element_type=F32) * (SCALE * LOG2E) + bias[...]
+        pair = kvh[:, g].reshape(keys, KV)
+        key_part, value_part = pair[:, :HD], pair[:, HD:]
+
+        def some_heads(i, _):
+            each = range(BATCH)
+            n = [part * heads + i * BATCH + j for j in each]
+            columns = [pl.ds(pl.multiple_of((g * GROUP + n[j]) * HD, HD), HD) for j in each]
+            query = jnp.concatenate([query_ref[:, columns[j]] for j in each], axis=0)
+            grad = jnp.concatenate([cot_ref[:, columns[j]] for j in each], axis=0)
+            below = pl.ds(pl.multiple_of(n[0] * rows, rows), BATCH * rows)
+            raw = lax.dot_general(query, key_part, NT, preferred_element_type=F32)
+            grad_prob = lax.dot_general(grad, value_part, NT, preferred_element_type=F32)
+            bias_all = jnp.concatenate([bias[...]] * BATCH, axis=0)
+            scores = raw * (SCALE * LOG2E) + bias_all
             weights = jnp.exp2(scores - jnp.max(scores, axis=1, keepdims=True))
             prob = weights * (1.0 / jnp.sum(weights, axis=1, keepdims=True))
             low = prob.astype(BF16)
-            att_ref[:, columns] = jnp.dot(low, value_part, preferred_element_type=F32).astype(BF16)
-            grad_prob = lax.dot_general(grad, value_part, NT, preferred_element_type=F32)
+            probs[below, :] = low
             inner = jnp.sum(prob * grad_prob, axis=1, keepdims=True)
             grad_score = (prob * (grad_prob - inner)).astype(BF16)
-            gq_ref[:, columns] = (jnp.dot(grad_score, key_part, preferred_element_type=F32) * SCALE).astype(BF16)
-            probs[below, :] = low
             grads[below, :] = grad_score
+            out = jnp.dot(low, value_part, preferred_element_type=F32).astype(BF16)
+            grad_out = (jnp.dot(grad_score, key_part, preferred_element_type=F32) * SCALE).astype(BF16)
+            for j in each:
+                att_ref[:, columns[j]] = out[j * rows : (j + 1) * rows]
+                gq_ref[:, columns[j]] = grad_out[j * rows : (j + 1) * rows]
             return 0
 
-        lax.fori_loop(0, heads, head, 0, unroll=UNROLL)
+        lax.fori_loop(0, heads // BATCH, some_heads, 0, unroll=UNROLL)
         if part == 0:
             return
         wide = pl.ds(g * GROUP * HD, GROUP * HD)
@@ -335,7 +347,7 @@
         for j in range(1, halo, 2):
             low, high = (j - 1) // 2, (j + 1) // 2
             links.send(c == 0, rim.at[g, j], rimx.at[g, low], rimx_recv.at[g, low], mate, tp)
-            links.send(c == 1, rim.at[g, j], rimx.at[g, high], rimx_recv.at[g, high], mate, tp)
+            links.send(c == 1, rim.at[g, j], rimx.at[g, high], rimx_recv.at[g, high], mate, tp, True)
 
     def rim_out(g):
         for i in range(half + 1):
@@ -393,7 +405,9 @@
             return 0
 
         lax.fori_loop(0, F // tile, outer, 0)
-        for q in range(chunks):
+
+    def grads_x(g, pieces):
+        for q in pieces:
             for k in range(1, X):
                 links.send(True, xsend.at[g, k - 1, cut(q)], xr.at[g, k - 1, cut(q)], x_recv.at[g, k - 1, q], at(z, (x + k) % X, c), tp)
 
@@ -419,8 +433,22 @@
             own32[g, cut(k), columns] = value
 
         pl.when(z == g)(lambda: fold(g, k, parts, keep))
-        pl.when(z != g)(lambda: fold(g, k, parts, send_low))
-        links.send(z != g, zs.at[g, cut(k)], zr.at[z, cut(k)], z_recv.at[z, k], at(g, x, c), tp)
+        if g in relayed:
+            pl.when(z != g)(lambda: fold(g, k, parts, send_low))
+            links.send(z != g, zs.at[g, cut(k)], zr.at[z, cut(k)], z_recv.at[z, k], at(g, x, c), tp)
+            return
+        for step, ends, passes in ((1, z == 0, (z > 0) & (z < g)), (-1, z == Z - 1, (z > g) & (z < Z - 1))):
+            def add():
+                links.arrive(za.at[g, cut(k)], a_recv.at[g, k], mate, tp)
+                fold(g, k, parts + [za.at[g]], send_low)
+
+            if (g if step > 0 else Z - 1 - g) > 0:
+                pl.when(ends)(lambda: fold(g, k, parts, send_low))
+                pl.when(passes)(add)
+                going = (z < g) if step > 0 else (z > g)
+                last = z + step == g
+                links.send(going & last, zs.at[g, cut(k)], zr.at[z, cut(k)], z_recv.at[z, k], at(z + step, x, c), tp)
+                links.send(going & (z + step != g), zs.at[g, cut(k)], za.at[g, cut(k)], a_recv.at[g, k], at(z + step, x, c), tp, True)
 
     first, second, third, fourth = order
     for k in range(chunks):
@@ -435,32 +463,34 @@
     weight_in(third, 0)
     weight_in(third, 1)
     project(second)
-    for k in range(2, chunks):
+    sum_pairs(first)
+    for k in range(2, chunks - 1):
         weight_in(third, k)
-        weight_x(third, k - 2)
-    weight_in(fourth, 0)
-    sum_pairs(first)
+    weight_x(third, 0)
     sum_pairs(second)
-    for k in range(1, max(chunks - 1, 2)):
-        weight_in(fourth, k)
-    for k in range(chunks - 2, chunks):
+    share_pairs(first)
+    for k in range(1, chunks // 2):
         weight_x(third, k)
-    share_pairs(first)
     await_pairs(first)
     attend(first, 0)
     for k in range(max(chunks - 1, 2), chunks):
+        weight_in(third, k)
+    for k in range(chunks // 2):
         weight_in(fourth, k)
-    for k in range(chunks - 1):
-        weight_x(fourth, k)
+        weight_x(third, chunks // 2 + k)
     share_pairs(second)
     attend(first, 1)
-    weight_x(fourth, chunks - 1)
+    for k in range(chunks // 2, chunks):
+        weight_in(fourth, k)
+        weight_x(fourth, k - chunks // 2)
     await_pairs(second)
     rim_out(first)
     attend(second, 0)
     project(third)
+    for k in range(chunks - chunks // 2, chunks):
+        weight_x(fourth, k)
+    rim_in(first)
     project(fourth)
-    rim_in(first)
     attend(second, 1)
     sum_pairs(third)
     sum_pairs(fourth)
@@ -468,16 +498,20 @@
     pair_grads(first)
     weight_grad(first)
     share_pairs(third)
+    grads_x(first, range(chunks // 2))
     await_pairs(third)
     attend(third, 0)
     share_pairs(fourth)
+    grads_x(first, range(chunks // 2, chunks))
     rim_in(second)
     attend(third, 1)
     pair_grads(second)
     weight_grad(second)
+    grads_x(second, range(chunks // 2))
     await_pairs(fourth)
     attend(fourth, 0)
     rim_out(third)
+    grads_x(second, range(chunks // 2, chunks))
     for k in range(chunks):
         rows_out(first, k)
     attend(fourth, 1)
@@ -485,11 +519,13 @@
     rim_in(third)
     pair_grads(third)
     weight_grad(third)
+    grads_x(third, range(chunks))
     for k in range(chunks):
         rows_out(second, k)
     rim_in(fourth)
     pair_grads(fourth)
     weight_grad(fourth)
+    grads_x(fourth, range(chunks))
 
     dkv_mine = jnp.concatenate([dkvall[g, c].reshape(R, KV) for g in range(KVH)], axis=1)
     dots[tp] = jnp.zeros((R, 128), F32)
@@ -501,7 +537,7 @@
         scaled = jnp.dot(dkv_mine, weight, preferred_element_type=F32) * (mask[:, columns].astype(F32) * DROP)
         wide = x_ref[:, columns].astype(F32)
         gains[0, :, columns] = jnp.sum(scaled * wide * inv_column, axis=0, keepdims=True)
-        upstream = scaled * gain_ref[:, columns].astype(F32)
+        upstream = scaled * gain_row[:, columns]
         ups[:, columns] = upstream
         upstream = upstream * wide
         total = upstream[:, :128]
@@ -520,13 +556,6 @@
         links.send(True, gains.at[2], gains.at[2 + k], gain_recv.at[2 + k], at((z + k) % Z, x, c), tp)
     for k in range(chunks):
         rows_out(third, k)
-    total = gains[2]
-    for k in range(1, Z):
-        links.arrive(gains.at[2 + k], gain_recv.at[2 + k], mate, tp)
-        total = total + gains[2 + k]
-    gains[2 + Z] = total
-    for k in range(1, X):
-        links.send(True, gains.at[2 + Z], gains.at[2 + Z + k], gain_recv.at[2 + Z + k], at(z, (x + k) % X, c), tp)
     for k in range(chunks):
         rows_out(fourth, k)
     for k in range(1, T):
@@ -546,6 +575,13 @@
 
     lax.fori_loop(0, R // strip, finish_rows, 0)
     put_out(ga_ref, ga_hbm)
+    total = gains[2]
+    for k in range(1, Z):
+        links.arrive(gains.at[2 + k], gain_recv.at[2 + k], mate, tp)
+        total = total + gains[2 + k]
+    gains[2 + Z] = total
+    for k in range(1, X):
+        links.send(True, gains.at[2 + Z], gains.at[2 + Z + k], gain_recv.at[2 + Z + k], at(z, (x + k) % X, c), tp)
     norm = (places * rows) ** (-0.5)
 
     for k in range(chunks):
@@ -553,9 +589,20 @@
             gw_ref[cut(k), columns] = value * norm
 
         sources = [(z + j) % Z for j in range(1, Z)]
-        for source in sources:
-            links.arrive(zr.at[source, cut(k)], z_recv.at[source, k], mate, tp)
-        fold(z, k, [zr.at[source] for source in sources], result)
+        ends = (z == 0) | (z == Z - 1)
+
+        def straight():
+            for source in sources:
+                links.arrive(zr.at[source, cut(k)], z_recv.at[source, k], mate, tp)
+            fold(z, k, [zr.at[source] for source in sources], result)
+
+        def beside():
+            for source in (z - 1, z + 1):
+                links.arrive(zr.at[source, cut(k)], z_recv.at[source, k], mate, tp)
+            fold(z, k, [zr.at[z - 1], zr.at[z + 1]], result)
+
+        pl.when(ends)(straight)
+        pl.when(jnp.logical_not(ends))(beside)
         put_out(gw_ref.at[cut(k)], gw_hbm.at[cut(k)])
     for k in range(1, X):
         links.arrive(gains.at[2 + Z + k], gain_recv.at[2 + Z + k], mate, tp)
@@ -575,6 +622,8 @@
     R = blocks * rows
     halo = 2 * -(-(DOC - 1) // (2 * rows))
     keys = rows * (halo + 1)
+    chunks = WR // 16
+    sends = chunks * (16 * X + 5) + 14 * (T - 1) + KVH * (2 * halo + 1) + X + 8
     shape = (S, T, X, Z, rows, F, WR, halo)
     vmem = pl.BlockSpec(memory_space=pltpu.VMEM)
     hbm = pl.BlockSpec(memory_space=pl.ANY)
@@ -620,13 +669,15 @@
             pltpu.VMEM((Z, X - 1, WR, F), BF16),
             pltpu.VMEM((Z, WR, F), BF16),
             pltpu.VMEM((Z, WR, F), BF16),
+            pltpu.VMEM((Z, WR, F), BF16),
             pltpu.VMEM((R, F), F32),
             pltpu.VMEM((2 + X + Z, 1, F), F32),
             pltpu.VMEM((GROUP * rows, keys), BF16),
             pltpu.VMEM((GROUP * rows, keys), BF16),
             pltpu.VMEM((rows, keys), F32),
-            dma((500,)),
-            dma((32,)),
+            pltpu.VMEM((1, F), F32),
+            dma((sends,)),
+            dma((5 + 2 * KVH + 1 + chunks,)),
             dma((S, WR // 16)),
             dma,
             dma((T,)),
@@ -639,12 +690,13 @@
             dma((KVH, T)),
             dma((Z, X, WR // 16)),
             dma((Z, WR // 16)),
+            dma((Z, WR // 16)),
             dma((2 + X + Z,)),
         ],
         compiler_params=pltpu.CompilerParams(collective_id=0, has_side_effects=True, vmem_limit_bytes=63 * 2**20),
     )(
         activations.reshape(R, F),
-        norm_gain.reshape(1, F),
+        norm_gain,
         keep_bits.reshape(R, F // 8),
         key_value_weight,
         queries[0],

time: 185 us -> 167 us (0.903)
  Pallas kernels: 174 us -> 159 us
    pallas_call x1, Pallas kernels: 174 us -> 159 us  [on_device(): pl.pallas_call(functools.partial(step_kernel, shape), in_specs=[hbm, vmem...]
where the time goes in v3:
time: 167 us
  Pallas kernels  159 us (95%)
  local copies, waits for them, and re-layouts  6.95 us (4%)
    pallas_call x1, Pallas kernels, on_device(): pl.pallas_call(functools.partial(step_kernel, shape), in_specs=[hbm, vmem...  159 us
    unnamed x13, local copies, waits for them, and re-layouts  6.95 us

profile of v3, /device:TPU:12, one launch (start us, length us, event | category | flops | bytes accessed | tf_op | source)
XLA Modules:
  0.0 166.7 jit_solution(15616148659596180651)
XLA Ops:
  0.6 159.1 %shard_map.110 = (bf16[128,4096]{1,0:T(8,128)(2,1)}, bf16[128,4096]{1,0:T(8,128)(2,1)}, bf16[256,4096]{1,0:T(8,128)(2,1)}, f32[64,4096]{1,0:T(8,128)}, f32[1,4096]{1,0:T(1,128)}) custom-call(bf16[256,4096]{1,0:T(8,128)(2,1)} %bitcast.9, bf16[4096]{0:T(1024)(128)(2,1)} %gain_ref.1, s32[256,512]{1,0:T(8,128)} %bitcast.15, bf16[64,4096]{1,0:T(8,128)(2,1)} %w_ref.1, ...), custom_call_target="tpu_custom_call" | custom-call | tf_op jit(solution)/shard_map/pallas_call | solution.py:632
  159.7 0.0 copy-start.2
  159.7 0.0 copy-start
  159.7 2.4 %copy.17 = bf16[1,128,4096]{2,1,0:T(8,128)(2,1)} copy(bf16[1,128,4096]{2,1,0:T(8,128)(2,1)} %bitcast.14) | data formatting | bytes 2097152
  162.2 0.0 copy-done.2
  162.2 1.0 copy.18
  163.1 0.0 copy-done
  163.2 0.0 copy-start.1
  163.2 1.3 copy.19
  164.5 0.6 copy-done.1
  165.1 0.0 copy-start.3
  165.1 1.0 copy.20
  166.1 0.0 copy-done.3
  166.1 0.6 copy.21
Async XLA Ops:
  159.7 2.5 %copy-start.2 = (bf16[128,4096]{1,0:T(8,128)(2,1)S(1)}, bf16[128,4096]{1,0:T(8,128)(2,1)}, u32[]{:S(2)}) copy-start(bf16[128,4096]{1,0:T(8,128)(2,1)} %get-tuple-element.11) | copy-start | bytes 3145732
  159.7 3.4 %copy-start = (bf16[256,4096]{1,0:T(8,128)(2,1)S(1)}, bf16[256,4096]{1,0:T(8,128)(2,1)}, u32[]{:S(2)}) copy-start(bf16[256,4096]{1,0:T(8,128)(2,1)} %get-tuple-element.12) | copy-start | bytes 6291460
  163.2 2.0 %copy-start.1 = (f32[64,4096]{1,0:T(8,128)S(1)}, f32[64,4096]{1,0:T(8,128)}, u32[]{:S(2)}) copy-start(f32[64,4096]{1,0:T(8,128)} %get-tuple-element.23) | copy-start | bytes 3145732
  165.1 1.0 copy-start.3

commit v4 on v3

--- a/solution.py
+++ b/solution.py
@@ -610,6 +610,20 @@
     gg_ref[...] = total * norm
     links.drain()
     for copy in results:
+        copy.wait()
+
+
+def hand_over(count, *refs):
+    sources, targets, buffers = refs[:count], refs[count : 2 * count], refs[2 * count : 3 * count]
+    in_sems, out_sems = refs[3 * count :]
+    coming = [pltpu.make_async_copy(sources[i], buffers[i], in_sems.at[i]) for i in range(count)]
+    going = [pltpu.make_async_copy(buffers[i], targets[i], out_sems.at[i]) for i in range(count)]
+    for copy in coming:
+        copy.start()
+    for i in range(count):
+        coming[i].wait()
+        going[i].start()
+    for copy in going:
         copy.wait()
 
 
@@ -703,6 +717,14 @@
         segment.reshape(S * T, rows),
         cotangent[0],
     )
+    out = pl.pallas_call(
+        functools.partial(hand_over, len(out)),
+        in_specs=[hbm] * len(out),
+        out_specs=[hbm] * len(out),
+        out_shape=[jax.ShapeDtypeStruct(o.shape, o.dtype) for o in out],
+        scratch_shapes=[pltpu.VMEM(o.shape, o.dtype) for o in out] + [dma((len(out),)), dma((len(out),))],
+        compiler_params=pltpu.CompilerParams(vmem_limit_bytes=60 * 2**20),
+    )(*out)
     attended, grad_queries, grad_activations, grad_weight, grad_gain = out
     return (
         attended[None],

time: 167 us -> 165 us (0.988)
  local copies, waits for them, and re-layouts: 6.95 us -> 0 us
  Pallas kernels: 159 us -> 163 us
    unnamed x13 -> x0, local copies, waits for them, and re-layouts: 6.95 us -> none
    pallas_call x0 -> x1, Pallas kernels: none -> 4.38 us  [on_device(): pl.pallas_call(functools.partial(hand_over, len(out)), in_specs=[hbm] * l...]
where the time goes in v4:
time: 165 us; the launch traced here: 164 us
  Pallas kernels  163 us (99%)
    pallas_call x1, Pallas kernels, on_device(): pl.pallas_call(functools.partial(step_kernel, shape), in_specs=[hbm, vmem...  159 us
    pallas_call x1, Pallas kernels, on_device(): pl.pallas_call(functools.partial(hand_over, len(out)), in_specs=[hbm] * l...  4.38 us

profile of v4, /device:TPU:12, one launch (start us, length us, event | category | flops | bytes accessed | tf_op | source)
XLA Modules:
  0.0 164.2 jit_solution(5319245879429506702)
XLA Ops:
  0.6 159.1 %shard_map.110 = (bf16[128,4096]{1,0:T(8,128)(2,1)}, bf16[128,4096]{1,0:T(8,128)(2,1)}, bf16[256,4096]{1,0:T(8,128)(2,1)}, f32[64,4096]{1,0:T(8,128)}, f32[1,4096]{1,0:T(1,128)}) custom-call(bf16[256,4096]{1,0:T(8,128)(2,1)} %bitcast.9, bf16[4096]{0:T(1024)(128)(2,1)} %gain_ref.1, s32[256,512]{1,0:T(8,128)} %bitcast.12, bf16[64,4096]{1,0:T(8,128)(2,1)} %w_ref.1, ...), custom_call_target="tpu_custom_call" | custom-call | tf_op jit(solution)/shard_map/pallas_call | solution.py:646
  159.7 4.4 %shard_map.111 = (bf16[128,4096]{1,0:T(8,128)(2,1)}, bf16[128,4096]{1,0:T(8,128)(2,1)}, bf16[256,4096]{1,0:T(8,128)(2,1)}, f32[64,4096]{1,0:T(8,128)}, f32[1,4096]{1,0:T(1,128)}) custom-call(bf16[128,4096]{1,0:T(8,128)(2,1)} %get-tuple-element.15.refs_0_, bf16[128,4096]{1,0:T(8,128)(2,1)} %get-tuple-element.16.refs_1_, ...), custom_call_target="tpu_custom_call" | custom-call | tf_op jit(solution)/shard_map/pallas_call | solution.py:720
